TPU v7x, 256 devices: a whole 4x4x8 slice. The times are simulated.
256 devices in a mesh: dp: 128 (over z, x, y), mp: 2 (over core).
Axes of the slice: x: 4, y: 4, z: 8, core: 2. Of those that a mesh axis runs over, the one named last changes fastest.
Arguments:
- embeddings: float32 [98304, 1024], P('dp', 'mp')
- cluster_id: int32 [98304], P('dp'), may hold values from 0 to 32767, as said below
- centroids: float32 [32768, 1024], P('dp', 'mp'), may hold values from -6 to 6
- cluster_mass: float32 [32768], P('dp'), may hold values from 1 to 16
Outputs:
- max_similarity: float32 [98304], P('dp')
- new_centroids: float32 [32768, 1024], P('dp', 'mp')
Inputs may be any that keep to these rules, and one draw needn't show every extreme that they name: `cluster_id`: cluster k belongs to owner k // 256. Among the 768 rows of one index of dp, at most 12 have clusters of any one owner, and for some owner exactly 12.
All inputs are finite; a program needn't handle non-finite values.
Results may differ from a plain program's by a relative error of at most 0.0011.
Values may be sent and summed in bfloat16 or wider, within the bound.
A program may use at most 64 MiB of HBM per device.

v0:
```python
import jax
import jax.numpy as jnp
from jax import lax
from jax.sharding import PartitionSpec as P

D = 1024


def gathered_total(value, axis):
    blocks = lax.all_gather(value, axis)
    return blocks.sum(axis=0)


def shards(embeddings, cluster_id, centroids, cluster_mass):
    owners = lax.axis_size("dp")
    row_count = embeddings.shape[0]
    slot_count = 2 * row_count
    capacity = slot_count // owners
    cluster_count = centroids.shape[0]
    squares = gathered_total(jnp.sum(embeddings * embeddings, axis=1), "mp")
    unit = (embeddings * lax.rsqrt(squares / D + 1e-06)[:, None]).astype(jnp.bfloat16)
    owner = cluster_id // cluster_count
    local = cluster_id - owner * cluster_count
    owner_hot = (owner[:, None] == jnp.arange(owners, dtype=jnp.int32)[None, :]).astype(
        jnp.bfloat16
    )
    row_index = jnp.arange(row_count, dtype=jnp.int32)
    lower = (row_index[:, None] >= row_index[None, :]).astype(jnp.bfloat16)
    running = jnp.dot(lower, owner_hot, preferred_element_type=jnp.float32)
    rank = jnp.sum(running * owner_hot.astype(jnp.float32), axis=1).astype(jnp.int32) - 1
    slot = owner * capacity + rank
    slot_index = jnp.arange(slot_count, dtype=jnp.int32)
    placed = slot_index[:, None] == slot[None, :]
    outgoing = jnp.dot(
        placed.astype(jnp.bfloat16), unit, preferred_element_type=jnp.float32
    ).astype(jnp.bfloat16)
    out_ids = jnp.max(jnp.where(placed, local[None, :] + 1, 0), axis=1) - 1
    incoming, in_ids = (
        lax.all_to_all(outgoing, "dp", split_axis=0, concat_axis=0, tiled=True),
        lax.all_to_all(out_ids, "dp", split_axis=0, concat_axis=0, tiled=True),
    )
    member = (jnp.arange(cluster_count, dtype=jnp.int32)[:, None] == in_ids[None, :]).astype(
        jnp.bfloat16
    )
    sums = jnp.dot(member, incoming, preferred_element_type=jnp.float32)
    counts = jnp.sum(member.astype(jnp.float32), axis=1)
    new_centroids = (cluster_mass[:, None] * centroids + sums) / (cluster_mass + counts)[:, None]
    half = slot_count // lax.axis_size("mp")
    start = lax.axis_index("mp") * half
    contract = (((1,), (1,)), ((), ()))
    gathered = lax.all_gather(incoming, "mp", axis=1, tiled=True)
    queries = lax.dynamic_slice_in_dim(gathered, start, half, 0)
    scores = lax.dot_general(queries, gathered, contract, preferred_element_type=jnp.float32)
    scores = scores / D
    query_ids = lax.dynamic_slice_in_dim(in_ids, start, half, 0)
    query_pos = start + jnp.arange(half, dtype=jnp.int32)
    same = (
        (query_ids[:, None] == in_ids[None, :])
        & (query_ids[:, None] >= 0)
        & (query_pos[:, None] != slot_index[None, :])
    )
    best = jnp.max(jnp.where(same, scores, -1.0), axis=1)
    best_all = lax.all_gather(best, "mp", axis=0, tiled=True)
    returned = lax.all_to_all(best_all, "dp", split_axis=0, concat_axis=0, tiled=True)
    max_similarity = jnp.take(returned, slot)
    return (max_similarity, new_centroids)


def solution(mesh):
    in_specs = (P("dp", "mp"), P("dp"), P("dp", "mp"), P("dp"))
    out_specs = (P("dp"), P("dp", "mp"))
    return jax.shard_map(shards, mesh=mesh, in_specs=in_specs, out_specs=out_specs, check_vma=False)
```

profile of v0, /device:TPU:1, one launch (start us, length us, event | category | flops | bytes accessed | tf_op | source)
XLA Modules:
  0.0 152.1 jit_solution(6354940080273488585)
XLA Ops:
  7.2 0.0 copy-start.1
  7.2 0.0 all-gather.5.cloned.1.call-start
  7.2 0.8 add_select_fusion
  8.0 0.4 fusion.11
  8.4 0.7 compare_select_fusion
  9.1 1.6 %multiply_reduce_fusion = f32[768]{0:T(1024)S(1)} fusion(f32[768,512]{1,0:T(8,128)} %param.4), kind=kLoop, calls=%fused_computation.17 | loop fusion | flops 785664 | bytes 1575936 | tf_op jit(solution)/shard_map/reduce_sum | solution.py:20
  10.7 4.7 %all-gather.1 = f32[2,1,768]{2,1,0:T(1,128)S(1)} all-gather(f32[1,1,768]{2,1,0:T(1,128)S(1)} %reshape.57), channel_id=2, replica_groups=mesh['dp'=128,'mp'=2] {'mp'}, dimensions={0}, use_global_device_ids=true | all-gather | bytes 9216 | tf_op jit(solution)/shard_map/all_gather | solution.py:10
  15.5 2.6 %fusion.2 = bf16[1536,512]{1,0:T(8,128)(2,1)} fusion(s32[768]{0:T(1024)S(1)} %get-tuple-element.3, f32[768,512]{1,0:T(8,128)S(1)} %copy-done.1, f32[768]{0:T(1024)S(1)} %add_rsqrt_fusion), kind=kOutput, calls=%fused_computation.7 | convolution fusion | flops 1210712064 | bytes 3151872 | tf_op jit(solution)/shard_map/dot_general | solution.py:34
  18.1 2.4 %all_to_all.24 = bf16[128,12,512]{2,1,0:T(8,128)(2,1)S(1)} reshape(bf16[1536,512]{1,0:T(8,128)(2,1)} %fusion.2) | data formatting | bytes 3145728 | tf_op jit(solution)/shard_map/all_to_all | solution.py:39
  20.4 63.9 %all_to_all.33 = bf16[128,12,512]{2,1,0:T(8,128)(2,1)} all-to-all(bf16[128,12,512]{2,1,0:T(8,128)(2,1)S(1)} %all_to_all.24), channel_id=1, replica_groups=mesh['dp'=128,'mp'=2] {'dp'}, dimensions={0} | all-to-all | bytes 3145728 | tf_op jit(solution)/shard_map/all_to_all | solution.py:39
  84.3 3.7 %all_to_all.26 = bf16[1536,512]{1,0:T(8,128)(2,1)} reshape(bf16[128,12,512]{2,1,0:T(8,128)(2,1)} %all_to_all.33) | data formatting | bytes 3145728 | tf_op jit(solution)/shard_map/all_to_all | solution.py:39
  88.0 0.0 all-gather.5.cloned.1.call-update
  88.0 0.7 select_reduce_fusion.1
  88.7 0.7 sub.23
  89.5 9.1 %all-to-all-start = ((s32[128,12,1]{1,2,0:T(1,128)}), s32[128,12,1]{1,2,0:T(1,128)S(1)}, u32[]{:S(2)}, u32[]{:S(2)}) async-start(s32[128,12,1]{1,2,0:T(1,128)} %bitcast), calls=%async_computation | async-start | bytes 131072 | tf_op jit(solution)/shard_map/all_to_all | solution.py:40
  98.6 10.7 %all-to-all-done = s32[128,12,1]{1,2,0:T(1,128)S(1)} async-done(((s32[128,12,1]{1,2,0:T(1,128)}), s32[128,12,1]{1,2,0:T(1,128)S(1)}, u32[]{:S(2)}, u32[]{:S(2)}) %all-to-all-start) | async-done | bytes 6176 | tf_op jit(solution)/shard_map/all_to_all | solution.py:40
  109.3 0.5 broadcast.78
  109.8 0.8 reduce.8
  110.6 0.1 all_to_all.23
  110.7 0.2 convert_reduce_fusion
  111.0 0.1 broadcast_compare_fusion
  111.1 5.8 %select_reduce_fusion = f32[768]{0:T(1024)S(1)} fusion(bf16[1536,1024]{1,0:T(8,128)(2,1)} %all-gather.5.cloned.1.call-done, s32[768]{0:T(1024)S(1)} %iota_add_fusion, s32[1536]{0:T(1024)S(1)} %all_to_all.23, s32[768]{0:T(1024)S(1)} %get-tuple-element.5, pred[768]{0:T(1024)(128)(4,1)S(1)} %get-tuple-element.4, s32[]{:T(128)S(6)} %select_n.28), kind=kOutput, calls=%fused_computation.1 | convolution fusion | flops 2424175872 | bytes 4734724 | tf_op jit(solution)/shard_map/dot_general | solution.py:53
  116.9 4.1 %all-gather.2 = f32[2,1,768]{2,1,0:T(1,128)S(1)} all-gather(f32[1,1,768]{2,1,0:T(1,128)S(1)} %reshape.59), channel_id=1, replica_groups=mesh['dp'=128,'mp'=2] {'mp'}, dimensions={0}, use_global_device_ids=true | all-gather | bytes 9216 | tf_op jit(solution)/shard_map/all_gather | solution.py:63
  121.0 0.7 all_to_all.27
  121.8 6.2 %all-to-all-start.2 = ((f32[128,12,1]{1,2,0:T(1,128)}), f32[128,12,1]{1,2,0:T(1,128)S(1)}, u32[]{:S(2)}, u32[]{:S(2)}) async-start(f32[128,12,1]{1,2,0:T(1,128)} %bitcast.1), calls=%async_computation.2 | async-start | bytes 131072 | tf_op jit(solution)/shard_map/all_to_all | solution.py:64
  128.0 1.4 fusion.9
  129.4 9.4 %all-to-all-done.2 = f32[128,12,1]{1,2,0:T(1,128)S(1)} async-done(((f32[128,12,1]{1,2,0:T(1,128)}), f32[128,12,1]{1,2,0:T(1,128)S(1)}, u32[]{:S(2)}, u32[]{:S(2)}) %all-to-all-start.2) | async-done | bytes 6176 | tf_op jit(solution)/shard_map/all_to_all | solution.py:64
  138.7 0.5 broadcast.79
  139.2 0.8 reduce.9
  140.1 0.1 all_to_all.29
  140.2 4.5 %gather_fusion = f32[768]{0:T(1024)S(1)} fusion(f32[1536]{0:T(1024)S(1)} %all_to_all.29, s32[1024]{0:T(1024)S(1)} %pad_clamp_fusion), kind=kCustom, calls=%fused_computation | custom fusion | bytes 9216 | tf_op jit(solution)/shard_map/jit(_take)/gather | solution.py:65
  144.6 0.6 and_select_fusion
  (17 shorter events, 0.1 us)
Async XLA Ops:
  7.2 8.3 %copy-start.1 = (f32[768,512]{1,0:T(8,128)S(1)}, f32[768,512]{1,0:T(8,128)}, u32[]{:S(2)}) copy-start(f32[768,512]{1,0:T(8,128)} %param.4) | copy-start | bytes 4718596
  7.2 103.9 %all-gather.5.cloned.1.call-start = ((), (), s32[]{:S(2)}) async-start(), calls=%async_computation.3 | async-start | bytes 4718592 | tf_op jit(solution)/shard_map/all_gather | solution.py:51
  88.0 23.0 %copy-start.2 = (f32[256]{0:T(256)S(1)}, f32[256]{0:T(256)}, u32[]{:S(2)}) copy-start(f32[256]{0:T(256)} %param.7) | copy-start | bytes 3076
  89.5 19.8 %all-to-all-start = ((s32[128,12,1]{1,2,0:T(1,128)}), s32[128,12,1]{1,2,0:T(1,128)S(1)}, u32[]{:S(2)}, u32[]{:S(2)}) async-start(s32[128,12,1]{1,2,0:T(1,128)} %bitcast), calls=%async_computation | async-start | bytes 131072 | tf_op jit(solution)/shard_map/all_to_all | solution.py:40
  111.1 16.9 %copy-start = (bf16[1536,512]{1,0:T(8,128)(2,1)S(1)}, bf16[1536,512]{1,0:T(8,128)(2,1)}, u32[]{:S(2)}) copy-start(bf16[1536,512]{1,0:T(8,128)(2,1)} %all_to_all.26) | copy-start | bytes 4718596
  111.1 16.9 %copy-start.3 = (f32[256,512]{1,0:T(8,128)S(1)}, f32[256,512]{1,0:T(8,128)}, u32[]{:S(2)}) copy-start(f32[256,512]{1,0:T(8,128)} %param.6) | copy-start | bytes 1572868
  121.8 16.9 %all-to-all-start.2 = ((f32[128,12,1]{1,2,0:T(1,128)}), f32[128,12,1]{1,2,0:T(1,128)S(1)}, u32[]{:S(2)}, u32[]{:S(2)}) async-start(f32[128,12,1]{1,2,0:T(1,128)} %bitcast.1), calls=%async_computation.2 | async-start | bytes 131072 | tf_op jit(solution)/shard_map/all_to_all | solution.py:64
Sparse Core Ops, SparseCore 0:
  88.1 15.2 all-gather.4
where the time goes:
time: 153 us; the launch traced here: 152 us
  blocking collectives  72.7 us (48%)
  waiting for transfers between devices  20 us (13%)
  starting transfers between devices  15.3 us (10%)
  between operations  14.2 us (9%)
  local copies, waits for them, and re-layouts  13.2 us (9%)
  matrix products  10.2 us (7%)
  other arithmetic  6.4 us (4%)
    all_to_all x1, blocking collectives, shards(): lax.all_to_all(outgoing, 'dp', split_axis=0, concat_axis=0, tiled=True)  63.9 us
    all_to_all x1, waiting for transfers between devices, shards(): lax.all_to_all(out_ids, 'dp', split_axis=0, concat_axis=0, tiled=True)  10.7 us
    all_to_all x1, waiting for transfers between devices, shards(): lax.all_to_all(best_all, 'dp', split_axis=0, concat_axis=0, tiled=True)  9.36 us
    all_to_all x1, starting transfers between devices, shards(): lax.all_to_all(out_ids, 'dp', split_axis=0, concat_axis=0, tiled=True)  9.13 us
    all_to_all x1, starting transfers between devices, shards(): lax.all_to_all(best_all, 'dp', split_axis=0, concat_axis=0, tiled=True)  6.17 us
    all_to_all x2, local copies, waits for them, and re-layouts, shards(): lax.all_to_all(outgoing, 'dp', split_axis=0, concat_axis=0, tiled=True)  6.01 us
    dot_general x1, matrix products, shards(): lax.dot_general(queries, gathered, contract, preferred_element_type=jnp.f...  5.78 us
    all_gather x1, blocking collectives, gathered_total(): blocks = lax.all_gather(value, axis)  4.68 us
  transfers between devices with their start and end apart: 3, of which 2 were waited for; matrix products, arithmetic and copies ran while one was open for 3% of the time, Pallas kernels for 0%

commit v1 on v0

v1 whole, which is shorter than its diff:
```python
import functools

import jax
import jax.numpy as jnp
from jax import lax
from jax.experimental import pallas as pl
from jax.experimental.pallas import tpu as pltpu
from jax.sharding import PartitionSpec as P

D = 1024
HALF = 512
ROWS = 768
CLUSTERS = 256
CAP = 12
ROOM = 128
NZ = 8
NXY = 16
GROUPS = (
    ((0, 1, 7), 16, 40),
    ((2, 6), 64, 24),
    ((3, 5), 96, 24),
    ((4,), 0, 16),
)
LANE = {k: base + CAP * m for members, base, _ in GROUPS for m, k in enumerate(members)}
KEYS = 128
MESH = pl.DeviceIdType.MESH
NT = (((1,), (1,)), ((), ()))
NEAR = (1, 7, 2, 6, 3, 5, 4)


def neg(d):
    return ((4 - d // 4) % 4) * 4 + (4 - d % 4) % 4


def hot(mask):
    return jnp.where(mask, 1.0, 0.0).astype(jnp.bfloat16)


def exchange_kernel(
    emb_ref, cid_ref, cent_ref, mass_ref,
    best_ref, nc_ref, flag_ref,
    emb, unit, sq_mine, sq_peer, zout, zin, mout, min_, xo0, xo1, xo2, xo3, idout,
    rows, rows_p, idin, idcol, tiles_i, best_out, ret1, ret2, cent, out_v,
    local_sem, sq_sem, zs, zr, ms, mr, xs, xr, ids_s, ids_r, ps, pr, bs, br, es, fs, fr,
):
    xout = (xo0, xo1, xo2, xo3)
    me = lax.axis_index("dp")
    c = lax.axis_index("mp")
    z, x, y = me // 16, (me // 4) % 4, me % 4

    def at_z(k):
        return (((z + k) % NZ) * 16 + x * 4 + y, c)

    def at_xy(d):
        return (z * 16 + ((x + d // 4) % 4) * 4 + (y + d % 4) % 4, c)

    partner = (me, 1 - c)

    load = pltpu.make_async_copy(emb_ref, emb, local_sem.at[0])
    load.start()
    cent_load = pltpu.make_async_copy(cent_ref, cent, local_sem.at[1])
    cent_load.start()
    blank = jnp.zeros((NXY, 16, HALF), jnp.bfloat16)
    rows[:, 48:64, :] = blank
    rows[:, 80:96, :] = blank
    rows[:, 112:128, :] = blank

    barrier = pltpu.get_barrier_semaphore()
    for k in range(1, NZ):
        pl.semaphore_signal(barrier, inc=1, device_id=at_z(k), device_id_type=MESH)
    for d in range(1, NXY):
        pl.semaphore_signal(barrier, inc=1, device_id=at_xy(d), device_id_type=MESH)
    pl.semaphore_signal(barrier, inc=1, device_id=partner, device_id_type=MESH)

    cid = cid_ref[...]
    owner = cid >> 8
    dz = ((owner >> 4) - z) & 7
    dxy = ((((owner >> 2) & 3) - x) & 3) * 4 + (((owner & 3) - y) & 3)
    target = dz * 16 + dxy
    lane128 = lax.broadcasted_iota(jnp.int32, (128, 128), 1)
    sub128 = lax.broadcasted_iota(jnp.int32, (128, 128), 0)
    upto = hot(sub128 <= lane128)
    sub8 = lax.broadcasted_iota(jnp.int32, (8, 128), 0)
    base_t = jnp.zeros((128, 128), jnp.float32)
    base_z = jnp.zeros((8, 128), jnp.float32)
    ranks, places = [], []
    for b in range(ROWS // 128):
        cut = slice(128 * b, 128 * b + 128)
        is_t = sub128 == target[:, cut]
        is_z = sub8 == dz[:, cut]
        run_t = base_t + jnp.dot(hot(is_t), upto, preferred_element_type=jnp.float32)
        run_z = base_z + jnp.dot(hot(is_z), upto, preferred_element_type=jnp.float32)
        ranks.append(jnp.sum(jnp.where(is_t, run_t, 0.0), axis=0, keepdims=True) - 1.0)
        places.append(jnp.sum(jnp.where(is_z, run_z, 0.0), axis=0, keepdims=True) - 1.0)
        base_t = jnp.broadcast_to(run_t[:, 127:128], (128, 128))
        base_z = jnp.broadcast_to(run_z[:, 127:128], (8, 128))
    most = jnp.max(base_z, axis=0, keepdims=True)
    over = jnp.where(most > float(ROOM), 1.0, 0.0)
    rank = jnp.concatenate(ranks, axis=1)
    place = jnp.concatenate(places, axis=1).astype(jnp.int32)
    slot = jnp.where(place < ROOM, dz * ROOM + place, -1)
    tile_of = dz * 16 + ((4 - (dxy >> 2)) & 3) * 4 + ((4 - (dxy & 3)) & 3)
    lane_of = rank.astype(jnp.int32)
    for k in range(NZ):
        lane_of = jnp.where(dz == k, lane_of + LANE[(NZ - k) % NZ], lane_of)
    tiles_i[...] = jnp.zeros_like(tiles_i)
    for b in range(ROWS // 128):
        cut = slice(128 * b, 128 * b + 128)
        tiles_i[0, b:b + 1, :] = tile_of[:, cut]
        tiles_i[1, b:b + 1, :] = lane_of[:, cut]
    row8 = lax.broadcasted_iota(jnp.int32, (8, ROWS), 0)
    values = jnp.where(
        row8 == 0, ((cid & 255) + 1).astype(jnp.float32),
        jnp.where(row8 == 1, dxy.astype(jnp.float32), jnp.where(row8 == 2, rank, 0.0)),
    ).astype(jnp.bfloat16)

    load.wait()
    squares = jnp.zeros((ROWS, 128), jnp.float32)
    for f in range(HALF // 128):
        part = emb[:, 128 * f:128 * f + 128]
        squares = squares + part * part
    mine = jnp.sum(squares.T, axis=0, keepdims=True)
    sq_mine[...] = mine
    pl.semaphore_wait(barrier, NZ - 1 + NXY - 1 + 1)
    sq_copy = pltpu.make_async_remote_copy(
        sq_mine, sq_peer, sq_sem.at[0], sq_sem.at[1], device_id=partner, device_id_type=MESH)
    sq_copy.start()

    place_hot = []
    for k in range(NZ):
        want = lax.broadcasted_iota(jnp.int32, (ROOM, ROWS), 0) + k * ROOM
        place_hot.append(hot(want == slot))
    meta_copies = []
    for k in (0,) + NEAR:
        meta = lax.dot_general(values, place_hot[k], NT, preferred_element_type=jnp.float32)
        meta = jnp.where(sub8 == 3, over, meta)
        if k == 0:
            min_[0] = meta
        else:
            mout[k] = meta
            copy = pltpu.make_async_remote_copy(
                mout.at[k], min_.at[NZ - k], ms.at[k], mr.at[NZ - k], device_id=at_z(k), device_id_type=MESH)
            copy.start()
            meta_copies.append((NZ - k, copy))

    sq_copy.wait()
    scale = lax.rsqrt((sq_mine[...] + sq_peer[...]) / D + 1e-06)
    scale = jnp.broadcast_to(scale, (128, ROWS)).T
    for f in range(HALF // 128):
        unit[:, 128 * f:128 * f + 128] = (emb[:, 128 * f:128 * f + 128] * scale).astype(jnp.bfloat16)

    z_copies = {}
    for k in NEAR + (0,):
        packed = jnp.dot(place_hot[k], unit[...], preferred_element_type=jnp.float32).astype(jnp.bfloat16)
        if k == 0:
            zin[0] = packed
        else:
            zout[k] = packed
            copy = pltpu.make_async_remote_copy(
                zout.at[k], zin.at[NZ - k], zs.at[k], zr.at[NZ - k], device_id=at_z(k), device_id_type=MESH)
            copy.start()
            z_copies[NZ - k] = copy
    meta_by = dict(meta_copies)

    def wait_meta(k):
        if k:
            meta_by[k].wait_recv()

    x_copies = {}

    def forward(g):
        members, base, count = GROUPS[g]
        total = None
        for m, k in enumerate(members):
            meta = min_[k]
            valid = meta[0:1, :] > 0.5
            there = jnp.where(valid, meta[1:2, :] * float(count) + meta[2:3, :] + float(CAP * m), -1.0)
            there = there.astype(jnp.int32)
            want = lax.broadcasted_iota(jnp.int32, (NXY * count, ROOM), 0)
            if k:
                z_copies[k].wait_recv()
            part = jnp.dot(hot(want == there), zin[k], preferred_element_type=jnp.float32)
            total = part if total is None else total + part
        for d in range(NXY):
            block = total[count * d:count * d + count, :].astype(jnp.bfloat16)
            if d == 0:
                rows[0, base:base + count, :] = block
            else:
                xout[g][d] = block
                copy = pltpu.make_async_remote_copy(
                    xout[g].at[d], rows.at[neg(d), pl.ds(base, count)], xs.at[g, d], xr.at[g, neg(d)],
                    device_id=at_xy(d), device_id_type=MESH)
                copy.start()
                x_copies[g, neg(d)] = copy

    p_copies = {}

    def share(g):
        _, base, count = GROUPS[g]
        for j in range(NXY):
            if j:
                x_copies[g, j].wait_recv()
            copy = pltpu.make_async_remote_copy(
                rows.at[j, pl.ds(base, count)], rows_p.at[j, pl.ds(base, count)], ps.at[g, j], pr.at[g, j],
                device_id=partner, device_id_type=MESH)
            copy.start()
            p_copies[g, j] = copy

    for k in GROUPS[0][0]:
        wait_meta(k)
    forward(0)

    for k in range(NZ):
        if k not in GROUPS[0][0]:
            wait_meta(k)
    ids = jnp.zeros((NXY, 128), jnp.float32)
    flag = jnp.zeros((1, 128), jnp.float32)
    sub16 = lax.broadcasted_iota(jnp.int32, (NXY, 128), 0)
    for k in range(NZ):
        meta = min_[k]
        valid = meta[0:1, :] > 0.5
        to = jnp.where(valid, meta[1:2, :], -1.0).astype(jnp.int32)
        place_k = meta[2:3, :].astype(jnp.int32) + LANE[k]
        left = jnp.where(sub16 == to, meta[0:1, :], 0.0).astype(jnp.bfloat16)
        ids = ids + lax.dot_general(left, hot(sub128 == place_k), NT, preferred_element_type=jnp.float32)
        flag = jnp.maximum(flag, meta[3:4, :])
    ids = jnp.where(lax.broadcasted_iota(jnp.int32, (NXY, 128), 1) == 127, flag, ids)
    id_copies = {}
    for d in range(NXY):
        if d == 0:
            idin[0] = ids[0:1, :]
        else:
            idout[d] = ids[d:d + 1, :]
            copy = pltpu.make_async_remote_copy(
                idout.at[d], idin.at[neg(d)], ids_s.at[d], ids_r.at[neg(d)], device_id=at_xy(d), device_id_type=MESH)
            copy.start()
            id_copies[neg(d)] = copy

    forward(1)
    share(0)
    for j in range(1, NXY):
        id_copies[j].wait_recv()
    flag = jnp.zeros((1, 128), jnp.float32)
    last = lax.broadcasted_iota(jnp.int32, (1, 128), 1) == 127
    for j in range(NXY):
        line = idin[j]
        flag = jnp.maximum(flag, jnp.where(last, line, 0.0))
        line = jnp.where(last | (line < 0.5), -1.0, line)
        idcol[j] = jnp.broadcast_to(line, (128, 128)).T
    flag_ref[...] = flag
    forward(2)
    share(1)
    forward(3)
    share(2)
    share(3)

    for g in range(4):
        for j in range(NXY):
            p_copies[g, j].wait_recv()

    for q in range(4):
        first = 8 * c + 2 * q
        query = rows[pl.ds(first, 2)].reshape(256, HALF)
        query_p = rows_p[pl.ds(first, 2)].reshape(256, HALF)
        id_q = [idin[first], idin[first + 1]]
        top = [jnp.full((8, 128), -float(D), jnp.float32) for _ in range(2)]

        def keys_step(t, top, first=first, q=q, query=query, query_p=query_p, id_q=id_q):
            j = (8 * c + t) % NXY
            scores = lax.dot_general(rows[j], query, NT, preferred_element_type=jnp.float32)
            scores = scores + lax.dot_general(rows_p[j], query_p, NT, preferred_element_type=jnp.float32)
            id_k = idcol[j]
            out = []
            for h in range(2):
                same = (id_k == id_q[h]) & ((sub128 != lane128) | (t != 2 * q + h))
                kept = jnp.where(same, scores[:, 128 * h:128 * h + 128], -float(D))
                out.append(jnp.maximum(top[h], jnp.max(kept.reshape(16, 8, 128), axis=0)))
            return tuple(out)

        top = lax.fori_loop(0, NXY, keys_step, tuple(top))
        for h in range(2):
            best_out[2 * q + h] = jnp.max(top[h], axis=0, keepdims=True) * (1.0 / D)

    def best_copy(i):
        jx, jy = 2 * c + i // 4, i % 4
        there = (z * 16 + ((x + jx) % 4) * 4 + (y + jy) % 4, c)
        return pltpu.make_async_remote_copy(
            best_out.at[i], ret1.at[8 * c + i], bs.at[i], br.at[i], device_id=there, device_id_type=MESH)

    @pl.when(c == 0)
    def _():
        ret1[0] = best_out[0]

    @pl.when(c == 1)
    def _():
        best_copy(0).start()

    for i in range(1, 8):
        best_copy(i).start()

    sub256 = lax.broadcasted_iota(jnp.int32, (CLUSTERS, 128), 0).astype(jnp.float32) + 1.0
    counts = jnp.zeros((CLUSTERS, 128), jnp.float32)
    sums = jnp.zeros((CLUSTERS, HALF), jnp.float32)
    for j in range(NXY):
        line = jnp.where(last, 0.0, idin[j])
        member = jnp.where(sub256 == line, 1.0, 0.0)
        counts = counts + member
        sums = sums + jnp.dot(member.astype(jnp.bfloat16), rows[j], preferred_element_type=jnp.float32)
    cent_load.wait()
    total = jnp.sum(counts, axis=1, keepdims=True)
    mass = jnp.broadcast_to(mass_ref[...], (128, CLUSTERS)).T[:, 0:1]
    cent[...] = (mass * cent[...] + sums) / (mass + total)
    nc_copy = pltpu.make_async_copy(cent, nc_ref, local_sem.at[2])
    nc_copy.start()

    @pl.when(c == 1)
    def _():
        best_copy(0).wait()

    for i in range(1, 8):
        best_copy(i).wait()
    half = pltpu.make_async_remote_copy(
        ret1.at[pl.ds(8 * c, 8)], ret1.at[pl.ds(8 * c, 8)], es.at[0], es.at[1], device_id=partner, device_id_type=MESH)
    half.start()
    half.wait()
    back = []
    for k in NEAR[::-1]:
        copy = pltpu.make_async_remote_copy(
            ret1, ret2.at[NZ - k], fs.at[k], fr.at[NZ - k], device_id=at_z(k), device_id_type=MESH)
        copy.start()
        back.append((NZ - k, copy))
    tile_t = tiles_i[0]
    lane_t = tiles_i[1]
    result = jnp.zeros((8, 128), jnp.float32)

    def pick(k, result):
        for j in range(NXY):
            line = ret1[j] if k == 0 else ret2[k, j]
            got = jnp.take_along_axis(
                jnp.broadcast_to(line, (8, 128)), lane_t, axis=1, mode="promise_in_bounds")
            result = jnp.where(tile_t == k * 16 + j, got, result)
        return result

    result = pick(0, result)
    for k, copy in back[::-1]:
        copy.wait_recv()
        result = pick(k, result)
    for b in range(ROWS // 128):
        best_ref[:, 128 * b:128 * b + 128] = result[b:b + 1, :]

    for _, copy in back:
        copy.wait_send()
    for _, copy in meta_copies:
        copy.wait_send()
    for copy in z_copies.values():
        copy.wait_send()
    for copy in x_copies.values():
        copy.wait_send()
    for copy in id_copies.values():
        copy.wait_send()
    for copy in p_copies.values():
        copy.wait_send()
    nc_copy.wait()


def compact(embeddings, cluster_id, centroids, cluster_mass):
    vmem = pl.BlockSpec(memory_space=pltpu.VMEM)
    anywhere = pl.BlockSpec(memory_space=pl.ANY)
    f32, bf16, i32 = jnp.float32, jnp.bfloat16, jnp.int32
    dma = pltpu.SemaphoreType.DMA
    return pl.pallas_call(
        exchange_kernel,
        out_shape=(
            jax.ShapeDtypeStruct((1, ROWS), f32),
            jax.ShapeDtypeStruct((CLUSTERS, HALF), f32),
            jax.ShapeDtypeStruct((1, 128), f32),
        ),
        in_specs=[anywhere, vmem, anywhere, vmem],
        out_specs=(vmem, anywhere, vmem),
        scratch_shapes=[
            pltpu.VMEM((ROWS, HALF), f32),
            pltpu.VMEM((ROWS, HALF), bf16),
            pltpu.VMEM((1, ROWS), f32),
            pltpu.VMEM((1, ROWS), f32),
            pltpu.VMEM((NZ, ROOM, HALF), bf16),
            pltpu.VMEM((NZ, ROOM, HALF), bf16),
            pltpu.VMEM((NZ, 8, 128), f32),
            pltpu.VMEM((NZ, 8, 128), f32),
            *[pltpu.VMEM((NXY, count, HALF), bf16) for _, _, count in GROUPS],
            pltpu.VMEM((NXY, 1, 128), f32),
            pltpu.VMEM((NXY, KEYS, HALF), bf16),
            pltpu.VMEM((NXY, KEYS, HALF), bf16),
            pltpu.VMEM((NXY, 1, 128), f32),
            pltpu.VMEM((NXY, 128, 128), f32),
            pltpu.VMEM((2, 8, 128), i32),
            pltpu.VMEM((8, 1, 128), f32),
            pltpu.VMEM((NXY, 1, 128), f32),
            pltpu.VMEM((NZ, NXY, 1, 128), f32),
            pltpu.VMEM((CLUSTERS, HALF), f32),
            pltpu.VMEM((8, 128), f32),
            dma((3,)), dma((2,)), dma((NZ,)), dma((NZ,)), dma((NZ,)), dma((NZ,)),
            dma((4, NXY)), dma((4, NXY)), dma((NXY,)), dma((NXY,)), dma((4, NXY)), dma((4, NXY)),
            dma((8,)), dma((8,)), dma((2,)), dma((NZ,)), dma((NZ,)),
        ],
        compiler_params=pltpu.CompilerParams(
            collective_id=0, has_side_effects=True, vmem_limit_bytes=48 * 2**20),
    )(embeddings, cluster_id.reshape(1, ROWS), centroids, cluster_mass.reshape(1, CLUSTERS))


def from_partner(value):
    return lax.ppermute(value, "mp", [(0, 1), (1, 0)])


def general(embeddings, cluster_id, centroids, cluster_mass):
    owners = lax.axis_size("dp")
    row_count = embeddings.shape[0]
    slot_count = 2 * row_count
    capacity = slot_count // owners
    cluster_count = centroids.shape[0]
    core = lax.axis_index("mp")
    squares = jnp.sum(embeddings * embeddings, axis=1)
    squares = squares + from_partner(squares)
    unit = (embeddings * lax.rsqrt(squares / D + 1e-06)[:, None]).astype(jnp.bfloat16)
    owner = cluster_id // cluster_count
    local = cluster_id - owner * cluster_count
    owner_hot = (owner[:, None] == jnp.arange(owners, dtype=jnp.int32)[None, :]).astype(jnp.bfloat16)
    row_index = jnp.arange(row_count, dtype=jnp.int32)
    lower = (row_index[:, None] >= row_index[None, :]).astype(jnp.bfloat16)
    running = jnp.dot(lower, owner_hot, preferred_element_type=jnp.float32)
    rank = jnp.sum(running * owner_hot.astype(jnp.float32), axis=1).astype(jnp.int32) - 1
    slot = owner * capacity + rank
    slot_index = jnp.arange(slot_count, dtype=jnp.int32)
    placed = slot_index[:, None] == slot[None, :]
    outgoing = jnp.dot(
        placed.astype(jnp.bfloat16), unit, preferred_element_type=jnp.float32
    ).astype(jnp.bfloat16)
    out_ids = jnp.max(jnp.where(placed, local[None, :] + 1, 0), axis=1) - 1
    incoming = lax.all_to_all(outgoing, "dp", split_axis=0, concat_axis=0, tiled=True)
    in_ids = lax.all_to_all(out_ids, "dp", split_axis=0, concat_axis=0, tiled=True)
    member = (jnp.arange(cluster_count, dtype=jnp.int32)[:, None] == in_ids[None, :]).astype(jnp.bfloat16)
    sums = jnp.dot(member, incoming, preferred_element_type=jnp.float32)
    counts = jnp.sum(member.astype(jnp.float32), axis=1)
    new_centroids = (cluster_mass[:, None] * centroids + sums) / (cluster_mass + counts)[:, None]
    half = slot_count // 2
    start = core * half
    contract = (((1,), (1,)), ((), ()))
    other = from_partner(incoming)
    scores = lax.dot_general(
        lax.dynamic_slice_in_dim(incoming, start, half, 0), incoming, contract, preferred_element_type=jnp.float32)
    scores = scores + lax.dot_general(
        lax.dynamic_slice_in_dim(other, start, half, 0), other, contract, preferred_element_type=jnp.float32)
    scores = scores / D
    query_ids = lax.dynamic_slice_in_dim(in_ids, start, half, 0)
    query_pos = start + jnp.arange(half, dtype=jnp.int32)
    same = (
        (query_ids[:, None] == in_ids[None, :])
        & (query_ids[:, None] >= 0)
        & (query_pos[:, None] != slot_index[None, :])
    )
    best = jnp.max(jnp.where(same, scores, -1.0), axis=1)
    best_p = from_partner(best)
    low, high = jnp.where(core == 0, best, best_p), jnp.where(core == 0, best_p, best)
    returned = lax.all_to_all(
        jnp.concatenate([low, high]), "dp", split_axis=0, concat_axis=0, tiled=True)
    return jnp.take(returned, slot), new_centroids


def shards(embeddings, cluster_id, centroids, cluster_mass):
    best, new_centroids, flag = compact(embeddings, cluster_id, centroids, cluster_mass)
    return lax.cond(
        flag[0, 127] > 0.5,
        lambda *args: general(*args),
        lambda *args: (best.reshape(ROWS), new_centroids),
        embeddings, cluster_id, centroids, cluster_mass,
    )


def solution(mesh):
    in_specs = (P("dp", "mp"), P("dp"), P("dp", "mp"), P("dp"))
    out_specs = (P("dp"), P("dp", "mp"))
    return jax.shard_map(shards, mesh=mesh, in_specs=in_specs, out_specs=out_specs, check_vma=False)
```

time: 153 us -> 85.4 us (0.56)
  Pallas kernels: 0 us -> 81.4 us
  blocking collectives: 72.7 us -> 0 us
  waiting for transfers between devices: 20 us -> 0 us
  starting transfers between devices: 15.3 us -> 0 us
  between operations: 14.2 us -> 1.37 us
  local copies, waits for them, and re-layouts: 13.2 us -> 2.24 us
  matrix products: 10.2 us -> 0 us
  other arithmetic: 6.4 us -> 0.02 us
    pallas_call x0 -> x1, Pallas kernels: none -> 81.4 us  [compact(): pl.pallas_call(exchange_kernel, out_shape=(jax.ShapeDtypeStruct((1, ROWS)...]
    all_to_all x1 -> x0, blocking collectives: 63.9 us -> none  [shards(): lax.all_to_all(outgoing, 'dp', split_axis=0, concat_axis=0, tiled=True)]
    all_to_all x2 -> x0, waiting for transfers between devices: 20 us -> none  [the longest x1 10.7 us: shards(): lax.all_to_all(out_ids, 'dp', split_axis=0, concat_axis=0, tiled=True)]
    all_to_all x2 -> x0, starting transfers between devices: 15.3 us -> none  [the longest x1 9.13 us: shards(): lax.all_to_all(out_ids, 'dp', split_axis=0, concat_axis=0, tiled=True)]
    dot_general x4 -> x0, matrix products: 10.2 us -> none  [the longest x1 5.78 us: shards(): lax.dot_general(queries, gathered, contract, preferred_element_type=jnp.f...]
    all_gather x2 -> x0, blocking collectives: 8.82 us -> none  [the longest x1 4.68 us: gathered_total(): blocks = lax.all_gather(value, axis)]
    all_to_all x7 -> x0, local copies, waits for them, and re-layouts: 7.96 us -> none  [the longest x2 6.01 us: shards(): lax.all_to_all(outgoing, 'dp', split_axis=0, concat_axis=0, tiled=True)]
    gather x1 -> x0, local copies, waits for them, and re-layouts: 4.46 us -> none  [shards(): max_similarity = jnp.take(returned, slot)]
  transfers between devices with their start and end apart: 3 -> 0, of which waited for: 2 -> 0; matrix products, arithmetic and copies ran while one was open for 3% -> 0% of each run, Pallas kernels for 0% -> 0%
where the time goes in v1:
time: 85.4 us; the launch traced here: 85.3 us
  Pallas kernels  81.4 us (95%)
  local copies, waits for them, and re-layouts  2.24 us (3%)
  between operations  1.37 us (2%)
    pallas_call x1, Pallas kernels, compact(): pl.pallas_call(exchange_kernel, out_shape=(jax.ShapeDtypeStruct((1, ROWS)...  81.4 us

profile of v1, /device:TPU:1, one launch (start us, length us, event | category | flops | bytes accessed | tf_op | source)
XLA Modules:
  0.0 85.3 jit_solution(5317805108485857536)
XLA Ops:
  0.6 0.0 copy-start
  0.6 0.0 copy-start.2
  0.7 0.0 copy-start.1
  0.7 0.0 copy-start.3
  0.7 0.8 reshape.58.cid_ref
  1.5 81.4 %shard_map.61 = (f32[1,768]{1,0:T(1,128)S(1)}, f32[256,512]{1,0:T(8,128)S(1)}, f32[1,128]{1,0:T(1,128)S(1)}) custom-call(f32[768,512]{1,0:T(8,128)} %emb_ref.1, s32[1,768]{1,0:T(1,128)S(1)} %reshape.58.cid_ref, f32[256,512]{1,0:T(8,128)} %cent_ref.1, f32[1,256]{1,0:T(1,128)} %bitcast.9), custom_call_target="tpu_custom_call" | custom-call | tf_op jit(solution)/shard_map/pallas_call | solution.py:371
  82.9 0.6 slice.3
  84.2 0.0 copy-done
  84.2 0.0 copy-done.2
  84.2 0.0 copy-done.1
  84.2 0.0 copy-done.3
  84.2 0.3 conditional.1
  84.5 0.0 copy-start.4
  84.5 0.8 copy.19
  85.3 0.0 copy-done.4
  (1 shorter events, 0.0 us)
Async XLA Ops:
  0.6 83.5 %copy-start = (f32[768,512]{1,0:T(8,128)S(1)}, f32[768,512]{1,0:T(8,128)}, u32[]{:S(2)}) copy-start(f32[768,512]{1,0:T(8,128)} %emb_ref.1) | copy-start | bytes 4718596
  0.6 83.5 %copy-start.2 = (s32[768]{0:T(1024)S(1)}, s32[768]{0:T(1024)}, u32[]{:S(2)}) copy-start(s32[768]{0:T(1024)} %param.7) | copy-start | bytes 9220
  0.7 83.5 %copy-start.1 = (f32[256,512]{1,0:T(8,128)S(1)}, f32[256,512]{1,0:T(8,128)}, u32[]{:S(2)}) copy-start(f32[256,512]{1,0:T(8,128)} %cent_ref.1) | copy-start | bytes 1572868
  0.7 83.5 %copy-start.3 = (f32[256]{0:T(256)S(1)}, f32[256]{0:T(256)}, u32[]{:S(2)}) copy-start(f32[256]{0:T(256)} %param.9) | copy-start | bytes 3076
  84.5 0.8 copy-start.4

commit v2 on v1

--- a/solution.py
+++ b/solution.py
@@ -17,12 +17,11 @@
 NXY = 16
 GROUPS = (
     ((0, 1, 7), 16, 40),
-    ((2, 6), 64, 24),
-    ((3, 5), 96, 24),
+    ((2, 6), 56, 24),
+    ((3, 5), 80, 24),
     ((4,), 0, 16),
 )
 LANE = {k: base + CAP * m for members, base, _ in GROUPS for m, k in enumerate(members)}
-KEYS = 128
 MESH = pl.DeviceIdType.MESH
 NT = (((1,), (1,)), ((), ()))
 NEAR = (1, 7, 2, 6, 3, 5, 4)
@@ -40,10 +39,12 @@
     emb_ref, cid_ref, cent_ref, mass_ref,
     best_ref, nc_ref, flag_ref,
     emb, unit, sq_mine, sq_peer, zout, zin, mout, min_, xo0, xo1, xo2, xo3, idout,
-    rows, rows_p, idin, idcol, tiles_i, best_out, ret1, ret2, cent, out_v,
+    r0, r1, r2, r3, p0, p1, p2, p3, idin, ik0, ik1, ik2, ik3, top0, top1, top2, top3, idq, sums,
+    tiles_i, column, best_out, ret1, ret2, cent,
     local_sem, sq_sem, zs, zr, ms, mr, xs, xr, ids_s, ids_r, ps, pr, bs, br, es, fs, fr,
 ):
     xout = (xo0, xo1, xo2, xo3)
+    rows, rows_p, idkey, top = (r0, r1, r2, r3), (p0, p1, p2, p3), (ik0, ik1, ik2, ik3), (top0, top1, top2, top3)
     me = lax.axis_index("dp")
     c = lax.axis_index("mp")
     z, x, y = me // 16, (me // 4) % 4, me % 4
@@ -60,10 +61,6 @@
     load.start()
     cent_load = pltpu.make_async_copy(cent_ref, cent, local_sem.at[1])
     cent_load.start()
-    blank = jnp.zeros((NXY, 16, HALF), jnp.bfloat16)
-    rows[:, 48:64, :] = blank
-    rows[:, 80:96, :] = blank
-    rows[:, 112:128, :] = blank
 
     barrier = pltpu.get_barrier_semaphore()
     for k in range(1, NZ):
@@ -169,7 +166,7 @@
     x_copies = {}
 
     def forward(g):
-        members, base, count = GROUPS[g]
+        members, _, count = GROUPS[g]
         total = None
         for m, k in enumerate(members):
             meta = min_[k]
@@ -184,11 +181,11 @@
         for d in range(NXY):
             block = total[count * d:count * d + count, :].astype(jnp.bfloat16)
             if d == 0:
-                rows[0, base:base + count, :] = block
+                rows[g][0] = block
             else:
                 xout[g][d] = block
                 copy = pltpu.make_async_remote_copy(
-                    xout[g].at[d], rows.at[neg(d), pl.ds(base, count)], xs.at[g, d], xr.at[g, neg(d)],
+                    xout[g].at[d], rows[g].at[neg(d)], xs.at[g, d], xr.at[g, neg(d)],
                     device_id=at_xy(d), device_id_type=MESH)
                 copy.start()
                 x_copies[g, neg(d)] = copy
@@ -196,12 +193,11 @@
     p_copies = {}
 
     def share(g):
-        _, base, count = GROUPS[g]
         for j in range(NXY):
             if j:
                 x_copies[g, j].wait_recv()
             copy = pltpu.make_async_remote_copy(
-                rows.at[j, pl.ds(base, count)], rows_p.at[j, pl.ds(base, count)], ps.at[g, j], pr.at[g, j],
+                rows[g].at[j], rows_p[g].at[j], ps.at[g, j], pr.at[g, j],
                 device_id=partner, device_id_type=MESH)
             copy.start()
             p_copies[g, j] = copy
@@ -246,40 +242,96 @@
         line = idin[j]
         flag = jnp.maximum(flag, jnp.where(last, line, 0.0))
         line = jnp.where(last | (line < 0.5), -1.0, line)
-        idcol[j] = jnp.broadcast_to(line, (128, 128)).T
+        turned = jnp.broadcast_to(line, (128, 128)).T
+        for g, (_, base, count) in enumerate(GROUPS):
+            idkey[g][count * j:count * j + count, :] = turned[base:base + count, :]
     flag_ref[...] = flag
+    for g, (_, _, count) in enumerate(GROUPS):
+        half = count * NXY // 2
+        for h in range(-(-half // 128)):
+            size = min(128, half - 128 * h)
+            block = idkey[g][pl.ds(pl.multiple_of(half * c + 128 * h, 8), size), :]
+            idq[g, :, 128 * h:128 * h + size] = block.T[0:8, :]
+        top[g][...] = jnp.full(top[g].shape, -float(D), jnp.float32)
+    sub256 = lax.broadcasted_iota(jnp.int32, (CLUSTERS, 128), 0).astype(jnp.float32) + 1.0
+
+    def member_sums(g):
+        count = GROUPS[g][2]
+        width = count * NXY
+        seen = jnp.zeros((CLUSTERS, 128), jnp.float32)
+        parts = []
+        for h in range(width // 128):
+            line = idkey[g][128 * h:128 * h + 128, :].T[0:1, :]
+            member = jnp.where(sub256 == line, 1.0, 0.0)
+            seen = seen + member
+            parts.append(member.astype(jnp.bfloat16))
+        return seen, jnp.dot(
+            jnp.concatenate(parts, axis=1), rows[g][...].reshape(width, HALF), preferred_element_type=jnp.float32)
+
+    def await_partner(g):
+        for j in range(NXY):
+            p_copies[g, j].wait_recv()
+
+    def score(kg, qg):
+        nk, nq = GROUPS[kg][2] * NXY, GROUPS[qg][2] * NXY // 2
+        first = pl.multiple_of((NXY // 2) * c, 8)
+        query = rows[qg][pl.ds(first, NXY // 2)].reshape(nq, HALF)
+        query_p = rows_p[qg][pl.ds(first, NXY // 2)].reshape(nq, HALF)
+        scores = lax.dot_general(rows[kg][...].reshape(nk, HALF), query, NT, preferred_element_type=jnp.float32)
+        scores = scores + lax.dot_general(
+            rows_p[kg][...].reshape(nk, HALF), query_p, NT, preferred_element_type=jnp.float32)
+        for h in range(-(-nq // 128)):
+            size = min(128, nq - 128 * h)
+            same = idkey[kg][...][:, :size] == idq[qg, 0:1, 128 * h:128 * h + size]
+            if kg == qg:
+                apart = lax.broadcasted_iota(jnp.int32, (nk, size), 0) - lax.broadcasted_iota(jnp.int32, (nk, size), 1)
+                same = same & (apart != nq * c + 128 * h)
+            kept = jnp.where(same, scores[:, 128 * h:128 * h + size], -float(D))
+            kept = jnp.max(kept.reshape(nk // 8, 8, size), axis=0)
+            old = top[qg][:, 128 * h:128 * h + size]
+            top[qg][:, 128 * h:128 * h + size] = jnp.maximum(old, kept)
+
+    counts, total = member_sums(0)
+    sums[...] = total
+    await_partner(0)
+    score(0, 0)
     forward(2)
     share(1)
+    more, total = member_sums(1)
+    counts = counts + more
+    sums[...] += total
+    await_partner(1)
+    score(0, 1)
+    score(1, 0)
+    score(1, 1)
     forward(3)
     share(2)
+    more, total = member_sums(2)
+    counts = counts + more
+    sums[...] += total
+    await_partner(2)
+    for g in range(2):
+        score(g, 2)
+        score(2, g)
+    score(2, 2)
     share(3)
-
-    for g in range(4):
-        for j in range(NXY):
-            p_copies[g, j].wait_recv()
-
-    for q in range(4):
-        first = 8 * c + 2 * q
-        query = rows[pl.ds(first, 2)].reshape(256, HALF)
-        query_p = rows_p[pl.ds(first, 2)].reshape(256, HALF)
-        id_q = [idin[first], idin[first + 1]]
-        top = [jnp.full((8, 128), -float(D), jnp.float32) for _ in range(2)]
-
-        def keys_step(t, top, first=first, q=q, query=query, query_p=query_p, id_q=id_q):
-            j = (8 * c + t) % NXY
-            scores = lax.dot_general(rows[j], query, NT, preferred_element_type=jnp.float32)
-            scores = scores + lax.dot_general(rows_p[j], query_p, NT, preferred_element_type=jnp.float32)
-            id_k = idcol[j]
-            out = []
-            for h in range(2):
-                same = (id_k == id_q[h]) & ((sub128 != lane128) | (t != 2 * q + h))
-                kept = jnp.where(same, scores[:, 128 * h:128 * h + 128], -float(D))
-                out.append(jnp.maximum(top[h], jnp.max(kept.reshape(16, 8, 128), axis=0)))
-            return tuple(out)
-
-        top = lax.fori_loop(0, NXY, keys_step, tuple(top))
-        for h in range(2):
-            best_out[2 * q + h] = jnp.max(top[h], axis=0, keepdims=True) * (1.0 / D)
+    await_partner(3)
+    for g in range(3):
+        score(g, 3)
+        score(3, g)
+    score(3, 3)
+    for g, (_, base, count) in enumerate(GROUPS):
+        half = count * NXY // 2
+        pieces = []
+        for h in range(-(-half // 128)):
+            size = min(128, half - 128 * h)
+            best = jnp.max(top[g][:, 128 * h:128 * h + size], axis=0, keepdims=True) * (1.0 / D)
+            pieces.append(jnp.broadcast_to(best, (128, size)).T)
+        best = jnp.concatenate(pieces, axis=0) if len(pieces) > 1 else pieces[0]
+        for i in range(NXY // 2):
+            column[i, base:base + count, :] = best[count * i:count * i + count, :]
+    for i in range(NXY // 2):
+        best_out[i] = column[i].T[0:1, :]
 
     def best_copy(i):
         jx, jy = 2 * c + i // 4, i % 4
@@ -298,18 +350,12 @@
     for i in range(1, 8):
         best_copy(i).start()
 
-    sub256 = lax.broadcasted_iota(jnp.int32, (CLUSTERS, 128), 0).astype(jnp.float32) + 1.0
-    counts = jnp.zeros((CLUSTERS, 128), jnp.float32)
-    sums = jnp.zeros((CLUSTERS, HALF), jnp.float32)
-    for j in range(NXY):
-        line = jnp.where(last, 0.0, idin[j])
-        member = jnp.where(sub256 == line, 1.0, 0.0)
-        counts = counts + member
-        sums = sums + jnp.dot(member.astype(jnp.bfloat16), rows[j], preferred_element_type=jnp.float32)
+    more, total = member_sums(3)
+    counts = counts + more
     cent_load.wait()
-    total = jnp.sum(counts, axis=1, keepdims=True)
+    number = jnp.sum(counts, axis=1, keepdims=True)
     mass = jnp.broadcast_to(mass_ref[...], (128, CLUSTERS)).T[:, 0:1]
-    cent[...] = (mass * cent[...] + sums) / (mass + total)
+    cent[...] = (mass * cent[...] + (sums[...] + total)) / (mass + number)
     nc_copy = pltpu.make_async_copy(cent, nc_ref, local_sem.at[2])
     nc_copy.start()
 
@@ -388,16 +434,19 @@
             pltpu.VMEM((NZ, 8, 128), f32),
             *[pltpu.VMEM((NXY, count, HALF), bf16) for _, _, count in GROUPS],
             pltpu.VMEM((NXY, 1, 128), f32),
-            pltpu.VMEM((NXY, KEYS, HALF), bf16),
-            pltpu.VMEM((NXY, KEYS, HALF), bf16),
+            *[pltpu.VMEM((NXY, count, HALF), bf16) for _, _, count in GROUPS],
+            *[pltpu.VMEM((NXY, count, HALF), bf16) for _, _, count in GROUPS],
             pltpu.VMEM((NXY, 1, 128), f32),
-            pltpu.VMEM((NXY, 128, 128), f32),
+            *[pltpu.VMEM((NXY * count, 128), f32) for _, _, count in GROUPS],
+            *[pltpu.VMEM((8, NXY // 2 * count), f32) for _, _, count in GROUPS],
+            pltpu.VMEM((4, 8, 384), f32),
+            pltpu.VMEM((CLUSTERS, HALF), f32),
             pltpu.VMEM((2, 8, 128), i32),
+            pltpu.VMEM((8, 128, 128), f32),
             pltpu.VMEM((8, 1, 128), f32),
             pltpu.VMEM((NXY, 1, 128), f32),
             pltpu.VMEM((NZ, NXY, 1, 128), f32),
             pltpu.VMEM((CLUSTERS, HALF), f32),
-            pltpu.VMEM((8, 128), f32),
             dma((3,)), dma((2,)), dma((NZ,)), dma((NZ,)), dma((NZ,)), dma((NZ,)),
             dma((4, NXY)), dma((4, NXY)), dma((NXY,)), dma((NXY,)), dma((4, NXY)), dma((4, NXY)),
             dma((8,)), dma((8,)), dma((2,)), dma((NZ,)), dma((NZ,)),

time: 85.4 us -> 67.8 us (0.79)
  Pallas kernels: 81.4 us -> 63.7 us
    pallas_call x1, Pallas kernels: 81.4 us -> 63.7 us  [compact(): pl.pallas_call(exchange_kernel, out_shape=(jax.ShapeDtypeStruct((1, ROWS)...]
where the time goes in v2:
time: 67.8 us; the launch traced here: 67.6 us
  Pallas kernels  63.7 us (94%)
  local copies, waits for them, and re-layouts  2.24 us (3%)
  between operations  1.37 us (2%)
    pallas_call x1, Pallas kernels, compact(): pl.pallas_call(exchange_kernel, out_shape=(jax.ShapeDtypeStruct((1, ROWS)...  63.7 us

profile of v2, /device:TPU:1, one launch (start us, length us, event | category | flops | bytes accessed | tf_op | source)
XLA Modules:
  0.0 67.6 jit_solution(16703239474911183411)
XLA Ops:
  0.6 0.0 copy-start
  0.6 0.0 copy-start.2
  0.7 0.0 copy-start.1
  0.7 0.0 copy-start.3
  0.7 0.8 %reshape.58.cid_ref = s32[1,768]{1,0:T(1,128)S(1)} reshape(s32[768]{0:T(1024)} %param.7) | data formatting | bytes 6144 | tf_op jit(solution)/shard_map/reshape | solution.py:456
  1.5 63.7 %shard_map.61 = (f32[1,768]{1,0:T(1,128)S(1)}, f32[256,512]{1,0:T(8,128)S(1)}, f32[1,128]{1,0:T(1,128)S(1)}) custom-call(f32[768,512]{1,0:T(8,128)} %emb_ref.1, s32[1,768]{1,0:T(1,128)S(1)} %reshape.58.cid_ref, f32[256,512]{1,0:T(8,128)} %cent_ref.1, f32[1,256]{1,0:T(1,128)} %bitcast.9), custom_call_target="tpu_custom_call" | custom-call | tf_op jit(solution)/shard_map/pallas_call | solution.py:417
  65.3 0.6 slice.3
  66.5 0.0 copy-done
  66.5 0.0 copy-done.2
  66.5 0.0 copy-done.1
  66.5 0.0 copy-done.3
  66.5 0.3 conditional.1
  66.8 0.0 copy-start.4
  66.8 0.8 %copy.19 = f32[256,512]{1,0:T(8,128)} copy(f32[256,512]{1,0:T(8,128)S(1)} %get-tuple-element.41) | data formatting | bytes 1048576
  67.6 0.0 copy-done.4
  (1 shorter events, 0.0 us)
Async XLA Ops:
  0.6 65.9 %copy-start = (f32[768,512]{1,0:T(8,128)S(1)}, f32[768,512]{1,0:T(8,128)}, u32[]{:S(2)}) copy-start(f32[768,512]{1,0:T(8,128)} %emb_ref.1) | copy-start | bytes 4718596
  0.6 65.9 %copy-start.2 = (s32[768]{0:T(1024)S(1)}, s32[768]{0:T(1024)}, u32[]{:S(2)}) copy-start(s32[768]{0:T(1024)} %param.7) | copy-start | bytes 9220
  0.7 65.9 %copy-start.1 = (f32[256,512]{1,0:T(8,128)S(1)}, f32[256,512]{1,0:T(8,128)}, u32[]{:S(2)}) copy-start(f32[256,512]{1,0:T(8,128)} %cent_ref.1) | copy-start | bytes 1572868
  0.7 65.9 %copy-start.3 = (f32[256]{0:T(256)S(1)}, f32[256]{0:T(256)}, u32[]{:S(2)}) copy-start(f32[256]{0:T(256)} %param.9) | copy-start | bytes 3076
  66.8 0.8 %copy-start.4 = (f32[768]{0:T(1024)}, f32[768]{0:T(1024)S(1)}, u32[]{:S(2)}) copy-start(f32[768]{0:T(1024)S(1)} %get-tuple-element.40) | copy-start | bytes 9220

commit v3 on v2

v3 whole, which is shorter than its diff:
```python
import functools

import jax
import jax.numpy as jnp
from jax import lax
from jax.experimental import pallas as pl
from jax.experimental.pallas import tpu as pltpu
from jax.sharding import PartitionSpec as P

D = 1024
HALF = 512
ROWS = 768
CLUSTERS = 256
CAP = 12
ROOM = 128
NZ = 8
NXY = 16
GROUPS = (((0, 1, 7), 0, 40), ((2, 6), 40, 24))
LANE = {k: base + CAP * m for members, base, _ in GROUPS for m, k in enumerate(members)}
FAR = (3, 5, 4)
FAR_SETS = (((3, 5), 0, 24, 2731, 16), ((4,), 2, 16, 1, 4))
WIDTH = tuple(count * NXY for _, _, count in GROUPS)
MESH = pl.DeviceIdType.MESH
NT = (((1,), (1,)), ((), ()))
NEAR = (1, 7, 2, 6)


def neg(d):
    return ((4 - d // 4) % 4) * 4 + (4 - d % 4) % 4


def hot(mask):
    return jnp.where(mask, 1.0, 0.0).astype(jnp.bfloat16)


def exchange_kernel(
    emb_ref, cid_ref, cent_ref, mass_ref,
    best_ref, nc_ref, flag_ref,
    emb, unit, sq_mine, sq_peer, zout, zin, z_far, z_far_p, mout, min_, xo0, xo1, idout, fo0, fo1, fi0, fi1, fid_out, fid_in,
    r0, r1, p0, p1, idin, ik0, ik1, ik_far, top, idq, acc0, acc1, acc_far, top_far, sums,
    tiles_i, column, best_out, far_out, ret1, ret2, far_z, back_out, far_ret, cent, cid_v, mass_v,
    local_sem, sq_sem, zs, zr, ms, mr, xs, xr, ids_s, ids_r, ps, pr, bs, br, fs, fr,
    ws, wr, vs, vr, us, ur, ts, tr,
):
    xout, rows, rows_p, idkey = (xo0, xo1), (r0, r1), (p0, p1), (ik0, ik1)
    fout, fin, acc = (fo0, fo1), (fi0, fi1), (acc0, acc1)
    me = lax.axis_index("dp")
    c = lax.axis_index("mp")
    z, x, y = me // 16, (me // 4) % 4, me % 4

    def at_z(k):
        return (((z + k) % NZ) * 16 + x * 4 + y, c)

    def at_xy(d):
        return (z * 16 + ((x + d // 4) % 4) * 4 + (y + d % 4) % 4, c)

    partner = (me, 1 - c)

    def send(src, dst, send_sem, recv_sem, to):
        copy = pltpu.make_async_remote_copy(src, dst, send_sem, recv_sem, device_id=to, device_id_type=MESH)
        copy.start()
        return copy

    cid_load = pltpu.make_async_copy(cid_ref, cid_v, local_sem.at[3])
    cid_load.start()
    mass_load = pltpu.make_async_copy(mass_ref, mass_v, local_sem.at[4])
    mass_load.start()
    load = pltpu.make_async_copy(emb_ref, emb, local_sem.at[0])
    load.start()
    cent_load = pltpu.make_async_copy(cent_ref, cent, local_sem.at[1])
    cent_load.start()
    barrier = pltpu.get_barrier_semaphore()
    for k in range(1, NZ):
        pl.semaphore_signal(barrier, inc=1, device_id=at_z(k), device_id_type=MESH)
    for d in range(1, NXY):
        pl.semaphore_signal(barrier, inc=1, device_id=at_xy(d), device_id_type=MESH)
        pl.semaphore_signal(barrier, inc=1, device_id=(at_xy(d)[0], 1 - c), device_id_type=MESH)
    for k in FAR:
        pl.semaphore_signal(barrier, inc=1, device_id=(at_z(k)[0], 1 - c), device_id_type=MESH)
    pl.semaphore_signal(barrier, inc=1, device_id=partner, device_id_type=MESH)

    cid_load.wait()
    cid = cid_v[...].reshape(1, ROWS)
    owner = cid >> 8
    dz = ((owner >> 4) - z) & 7
    dxy = ((((owner >> 2) & 3) - x) & 3) * 4 + (((owner & 3) - y) & 3)
    target = dz * 16 + dxy
    lane128 = lax.broadcasted_iota(jnp.int32, (128, 128), 1)
    sub128 = lax.broadcasted_iota(jnp.int32, (128, 128), 0)
    upto = hot(sub128 <= lane128)
    sub8 = lax.broadcasted_iota(jnp.int32, (8, 128), 0)
    sub16 = lax.broadcasted_iota(jnp.int32, (NXY, 128), 0)
    last = lax.broadcasted_iota(jnp.int32, (1, 128), 1) == 127
    base_t = jnp.zeros((128, 128), jnp.float32)
    base_z = jnp.zeros((8, 128), jnp.float32)
    ranks, places = [], []
    for b in range(ROWS // 128):
        cut = slice(128 * b, 128 * b + 128)
        is_t = sub128 == target[:, cut]
        is_z = sub8 == dz[:, cut]
        run_t = base_t + jnp.dot(hot(is_t), upto, preferred_element_type=jnp.float32)
        run_z = base_z + jnp.dot(hot(is_z), upto, preferred_element_type=jnp.float32)
        ranks.append(jnp.sum(jnp.where(is_t, run_t, 0.0), axis=0, keepdims=True) - 1.0)
        places.append(jnp.sum(jnp.where(is_z, run_z, 0.0), axis=0, keepdims=True) - 1.0)
        base_t = jnp.broadcast_to(run_t[:, 127:128], (128, 128))
        base_z = jnp.broadcast_to(run_z[:, 127:128], (8, 128))
    near_most = jnp.where((sub8 < 3) | (sub8 > 5), base_z, 0.0)
    over = jnp.where(jnp.max(near_most, axis=0, keepdims=True) > float(ROOM), 1.0, 0.0)
    rank_f = jnp.concatenate(ranks, axis=1)
    rank = rank_f.astype(jnp.int32)
    place = jnp.concatenate(places, axis=1).astype(jnp.int32)
    slot = jnp.where(place < ROOM, dz * ROOM + place, -1)
    far_row = (dz >= 3) & (dz <= 5)
    far_lane = jnp.where(dz == 3, rank, jnp.where(dz == 5, rank + CAP, rank + 2 * CAP))
    far_lane = jnp.where(far_row, far_lane, -1)
    far_slot = (
        jnp.where((dz == 3) | (dz == 5), dxy * FAR_SETS[0][2] + far_lane, -1),
        jnp.where(dz == 4, dxy * FAR_SETS[1][2] + rank, -1),
    )
    turned = ((4 - (dxy >> 2)) & 3) * 4 + ((4 - (dxy & 3)) & 3)
    tile_of = jnp.where(far_row, NZ * NXY + dxy, dz * NXY + turned)
    lane_of = jnp.where(far_row, far_lane, rank)
    for k in (0,) + NEAR:
        lane_of = jnp.where(dz == k, rank + LANE[(NZ - k) % NZ], lane_of)
    tiles_i[...] = jnp.zeros_like(tiles_i)
    for b in range(ROWS // 128):
        cut = slice(128 * b, 128 * b + 128)
        tiles_i[0, b:b + 1, :] = tile_of[:, cut]
        tiles_i[1, b:b + 1, :] = lane_of[:, cut]
    row8 = lax.broadcasted_iota(jnp.int32, (8, ROWS), 0)
    local = ((cid & 255) + 1).astype(jnp.float32)
    values = jnp.where(
        row8 == 0, local,
        jnp.where(row8 == 1, dxy.astype(jnp.float32), jnp.where(row8 == 2, rank_f, 0.0)),
    ).astype(jnp.bfloat16)

    load.wait()
    squares = jnp.zeros((ROWS, 128), jnp.float32)
    for f in range(HALF // 128):
        part = emb[:, 128 * f:128 * f + 128]
        squares = squares + part * part
    mine = jnp.sum(squares.T, axis=0, keepdims=True)
    sq_mine[...] = mine
    pl.semaphore_wait(barrier, NZ - 1 + 2 * (NXY - 1) + len(FAR) + 1)
    sq_copy = send(sq_mine, sq_peer, sq_sem.at[0], sq_sem.at[1], partner)

    place_hot = {}
    for k in (0,) + NEAR:
        want = lax.broadcasted_iota(jnp.int32, (ROOM, ROWS), 0) + k * ROOM
        place_hot[k] = hot(want == slot)
    far_hot = [
        hot(lax.broadcasted_iota(jnp.int32, (NXY * count, ROWS), 0) == far_slot[e])
        for e, (_, _, count, _, _) in enumerate(FAR_SETS)
    ]

    sq_copy.wait()
    scale = lax.rsqrt((sq_mine[...] + sq_peer[...]) / D + 1e-06)
    scale = jnp.broadcast_to(scale, (128, ROWS)).T
    for f in range(HALF // 128):
        unit[:, 128 * f:128 * f + 128] = (emb[:, 128 * f:128 * f + 128] * scale).astype(jnp.bfloat16)

    z_copies, meta_copies, f_copies, fid_copies = {}, {}, {}, {}

    def pack(k):
        packed = jnp.dot(place_hot[k], unit[...], preferred_element_type=jnp.float32).astype(jnp.bfloat16)
        if k == 0:
            zin[0] = packed
        else:
            zout[k] = packed
            z_copies[NZ - k] = send(zout.at[k], zin.at[NZ - k], zs.at[k], zr.at[NZ - k], at_z(k))

    pack(1)
    pack(7)
    left = jnp.where(
        far_row & (lax.broadcasted_iota(jnp.int32, (NXY, ROWS), 0) == dxy), local, 0.0).astype(jnp.bfloat16)
    right = hot(lax.broadcasted_iota(jnp.int32, (128, ROWS), 0) == far_lane)
    ids = lax.dot_general(left, right, NT, preferred_element_type=jnp.float32)
    for d in range(NXY):
        if d == 0:
            fid_in[0] = ids[0:1, :]
        else:
            fid_out[d] = ids[d:d + 1, :]
            fid_copies[neg(d)] = send(fid_out.at[d], fid_in.at[neg(d)], vs.at[d], vr.at[neg(d)], at_xy(d))

    def pack_far(e):
        count = FAR_SETS[e][2]
        packed = jnp.dot(far_hot[e], unit[...], preferred_element_type=jnp.float32)
        for d in range(NXY):
            block = packed[count * d:count * d + count, :].astype(jnp.bfloat16)
            if d == 0:
                fin[e][0] = block
            else:
                fout[e][d] = block
                f_copies[e, neg(d)] = send(
                    fout[e].at[d], fin[e].at[neg(d)], ws.at[e, d], wr.at[e, neg(d)], at_xy(d))

    pack_far(0)
    pack_far(1)
    for k in NEAR + (0,):
        meta = lax.dot_general(values, place_hot[k], NT, preferred_element_type=jnp.float32)
        if k == 0:
            min_[0] = meta
        else:
            mout[k] = meta
            meta_copies[NZ - k] = send(mout.at[k], min_.at[NZ - k], ms.at[k], mr.at[NZ - k], at_z(k))
    pack(2)
    pack(6)
    pack(0)

    x_copies, p_copies = {}, {}

    def forward(g):
        members, _, count = GROUPS[g]
        total = None
        for m, k in enumerate(members):
            if g == 0 and k:
                meta_copies[k].wait_recv()
            meta = min_[k]
            valid = meta[0:1, :] > 0.5
            there = jnp.where(valid, meta[1:2, :] * float(count) + meta[2:3, :] + float(CAP * m), -1.0)
            there = there.astype(jnp.int32)
            want = lax.broadcasted_iota(jnp.int32, (NXY * count, ROOM), 0)
            if k:
                z_copies[k].wait_recv()
            part = jnp.dot(hot(want == there), zin[k], preferred_element_type=jnp.float32)
            total = part if total is None else total + part
        for d in range(NXY):
            block = total[count * d:count * d + count, :].astype(jnp.bfloat16)
            if d == 0:
                rows[g][0] = block
            else:
                xout[g][d] = block
                x_copies[g, neg(d)] = send(
                    xout[g].at[d], rows[g].at[neg(d)], xs.at[g, d], xr.at[g, neg(d)], at_xy(d))

    def share(g):
        for j in range(NXY):
            if j:
                x_copies[g, j].wait_recv()
            p_copies[g, j] = send(rows[g].at[j], rows_p[g].at[j], ps.at[g, j], pr.at[g, j], partner)

    def share_far(kk):
        z_copies[FAR[kk]].wait_recv()
        p_copies[2 + kk, 0] = send(z_far.at[kk], z_far_p.at[kk], ps.at[2 + kk, 0], pr.at[2 + kk, 0], partner)

    for j in range(1, NXY):
        fid_copies[j].wait_recv()
    known = jnp.concatenate([fid_in[j] for j in range(NXY)], axis=0).astype(jnp.bfloat16)
    back_at = jnp.zeros((NXY, 128), jnp.float32)
    far_values, far_places = [], []
    for planes, first, count, factor, shift in FAR_SETS:
        width = NXY * count
        flat = lax.broadcasted_iota(jnp.int32, (1, width), 1)
        holder = (flat * factor) >> shift
        within = flat - holder * count
        lane = jnp.where(within < CAP * len(planes), within + CAP * first, -1)
        spread = hot(lax.broadcasted_iota(jnp.int32, (128, width), 0) == lane)
        mine16 = lax.broadcasted_iota(jnp.int32, (NXY, width), 0) == holder
        far_ids = jnp.dot(known, spread, preferred_element_type=jnp.float32)
        far_ids = jnp.sum(jnp.where(mine16, far_ids, 0.0), axis=0, keepdims=True)
        low = lax.broadcasted_iota(jnp.int32, (8, width), 0) * CAP
        inside = (within >= low) & (within < low + CAP) & (low < CAP * len(planes)) & (far_ids > 0.5)
        base_f = jnp.zeros((8, 128), jnp.float32)
        runs = []
        for b in range(width // 128):
            run = base_f + jnp.dot(hot(inside[:, 128 * b:128 * b + 128]), upto, preferred_element_type=jnp.float32)
            runs.append(run)
            base_f = jnp.broadcast_to(run[:, 127:128], (8, 128))
        over = jnp.maximum(over, jnp.where(jnp.max(base_f, axis=0, keepdims=True) > float(ROOM), 1.0, 0.0))
        far_place = jnp.where(inside, jnp.concatenate(runs, axis=1) - 1.0, -1.0)
        far_place = jnp.where(far_place < float(ROOM), far_place, -1.0)
        any_place = jnp.maximum(jnp.max(far_place, axis=0, keepdims=True), 0.0)
        back_at = back_at + lax.dot_general(
            jnp.where(mine16, any_place, 0.0).astype(jnp.bfloat16), spread, NT, preferred_element_type=jnp.float32)
        far_values.append(jnp.broadcast_to(far_ids, (8, width)).astype(jnp.bfloat16))
        far_places.append(far_place)
    back_at = back_at.astype(jnp.int32)

    def relay_far(e):
        planes, _, count, _, _ = FAR_SETS[e]
        width = NXY * count
        chosen = []
        for m, k in enumerate(planes):
            want = lax.broadcasted_iota(jnp.int32, (ROOM, width), 0).astype(jnp.float32)
            chosen.append(hot(want == far_places[e][m:m + 1, :]))
            mout[k] = lax.dot_general(far_values[e], chosen[m], NT, preferred_element_type=jnp.float32)
            meta_copies[NZ - k] = send(mout.at[k], min_.at[NZ - k], ms.at[k], mr.at[NZ - k], at_z(k))
        for j in range(1, NXY):
            f_copies[e, j].wait_recv()
        for m, k in enumerate(planes):
            zout[k] = jnp.dot(
                chosen[m], fin[e][...].reshape(width, HALF), preferred_element_type=jnp.float32).astype(jnp.bfloat16)
            z_copies[NZ - k] = send(
                zout.at[k], z_far.at[FAR.index(NZ - k)], zs.at[k], zr.at[NZ - k], at_z(k))

    forward(0)
    relay_far(0)

    for k in (2, 6):
        meta_copies[k].wait_recv()
    ids = jnp.zeros((NXY, 128), jnp.float32)
    for k in (0,) + NEAR:
        meta = min_[k]
        valid = meta[0:1, :] > 0.5
        to = jnp.where(valid, meta[1:2, :], -1.0).astype(jnp.int32)
        place_k = meta[2:3, :].astype(jnp.int32) + LANE[k]
        left = jnp.where(sub16 == to, meta[0:1, :], 0.0).astype(jnp.bfloat16)
        ids = ids + lax.dot_general(left, hot(sub128 == place_k), NT, preferred_element_type=jnp.float32)
    id_copies = {}
    for d in range(NXY):
        if d == 0:
            idin[0] = ids[0:1, :]
        else:
            idout[d] = ids[d:d + 1, :]
            id_copies[neg(d)] = send(idout.at[d], idin.at[neg(d)], ids_s.at[d], ids_r.at[neg(d)], at_xy(d))

    forward(1)
    relay_far(1)

    share(0)
    for j in range(1, NXY):
        id_copies[j].wait_recv()
    for j in range(NXY):
        line = idin[j]
        line = jnp.where(line < 0.5, -1.0, line)
        turned = jnp.broadcast_to(line, (128, 128)).T
        for g, (_, base, count) in enumerate(GROUPS):
            idkey[g][count * j:count * j + count, :] = turned[base:base + count, :]

    for g in range(2):
        half = WIDTH[g] // 2
        for h in range(-(-half // 128)):
            size = min(128, half - 128 * h)
            block = idkey[g][pl.ds(pl.multiple_of(half * c + 128 * h, 8), size), :]
            idq[g, :, 128 * h:128 * h + size] = block.T[0:8, :]
    for ref in (top, top_far, acc0, acc1, acc_far):
        ref[...] = jnp.full(ref.shape, -float(D), jnp.float32)
    sub256 = lax.broadcasted_iota(jnp.int32, (CLUSTERS, 128), 0).astype(jnp.float32) + 1.0

    def member_sums(source, key):
        seen = jnp.zeros((CLUSTERS, 128), jnp.float32)
        parts = []
        for h in range(key.shape[0] // 128):
            line = source[128 * h:128 * h + 128, :].T[0:1, :]
            member = jnp.where(sub256 == line, 1.0, 0.0)
            seen = seen + member
            parts.append(member.astype(jnp.bfloat16))
        member = jnp.concatenate(parts, axis=1) if len(parts) > 1 else parts[0]
        return seen, jnp.dot(member, key, preferred_element_type=jnp.float32)

    def near_sums(g):
        return member_sums(idkey[g], rows[g][...].reshape(WIDTH[g], HALF))

    def keys_of(g):
        return rows[g][...].reshape(WIDTH[g], HALF), rows_p[g][...].reshape(WIDTH[g], HALF)

    def own_half(g):
        half = WIDTH[g] // 2
        first = pl.ds(pl.multiple_of(NXY // 2 * c, 8), NXY // 2)
        return rows[g][first].reshape(half, HALF), rows_p[g][first].reshape(half, HALF)

    def nt(a, b):
        return lax.dot_general(a, b, NT, preferred_element_type=jnp.float32)

    def score_near(e):
        pairs = [(e, e)] + [pair for g in range(e) for pair in ((g, e), (e, g))]
        own = [nt(keys_of(kg)[0], own_half(qg)[0]) for kg, qg in pairs]
        for j in range(NXY):
            p_copies[e, j].wait_recv()
        for (kg, qg), part in zip(pairs, own):
            nk, nq = WIDTH[kg], WIDTH[qg] // 2
            scores = part + nt(keys_of(kg)[1], own_half(qg)[1])
            for h in range(-(-nq // 128)):
                cut = slice(128 * h, min(128 * h + 128, nq))
                size = cut.stop - cut.start
                same = idkey[kg][...][:, :size] == idq[qg, 0:1, cut]
                if kg == qg:
                    apart = (lax.broadcasted_iota(jnp.int32, (nk, size), 0)
                             - lax.broadcasted_iota(jnp.int32, (nk, size), 1))
                    same = same & (apart != nq * c + 128 * h)
                kept = jnp.where(same, scores[:, cut], -float(D))
                top[qg, :, cut] = jnp.maximum(top[qg, :, cut], jnp.max(kept.reshape(nk // 8, 8, size), axis=0))

    half_far = pl.ds(pl.multiple_of(ROOM // 2 * c, ROOM // 2), ROOM // 2)

    def score_far(planes):
        first, width = planes[0], ROOM * len(planes)
        cut = slice(first, first + len(planes))
        groups = [0, 1] + [2 + kk for kk in range(first + len(planes))]

        def side(g):
            if g < 2:
                return own_half(g)
            return z_far[g - 2, half_far, :], z_far_p[g - 2, half_far, :]

        columns = z_far[cut].reshape(width, HALF)
        own = [nt(side(g)[0], columns) for g in groups]
        for kk in planes:
            p_copies[2 + kk, 0].wait_recv()
        columns = z_far_p[cut].reshape(width, HALF)
        for g, part in zip(groups, own):
            scores = part + nt(side(g)[1], columns)
            n = scores.shape[0]
            if g < 2:
                mine = idkey[g][pl.ds(pl.multiple_of(n * c, 8), n), :]
            else:
                mine = ik_far[g - 2, half_far, :]
            for kk in planes:
                line = min_[FAR[kk]][0:1, :]
                same = mine == line
                if g == 2 + kk:
                    apart = (lax.broadcasted_iota(jnp.int32, (n, ROOM), 1)
                             - lax.broadcasted_iota(jnp.int32, (n, ROOM), 0))
                    same = same & (apart != n * c)
                kept = jnp.where(same, scores[:, ROOM * (kk - first):ROOM * (kk - first) + ROOM], -float(D))
                top_far[kk] = jnp.maximum(top_far[kk], jnp.max(kept.reshape(n // 8, 8, ROOM), axis=0))
                if g < 2:
                    acc[g][...] = jnp.maximum(acc[g][...], kept)
                elif g - 2 < first:
                    acc_far[g - 2] = jnp.maximum(acc_far[g - 2], kept)

    def take_far(kk):
        meta_copies[FAR[kk]].wait_recv()
        line = min_[FAR[kk]][0:1, :]
        ik_far[kk] = jnp.broadcast_to(jnp.where(line < 0.5, -1.0, line), (128, 128)).T
        share_far(kk)

    counts, total = near_sums(0)
    sums[...] = total
    score_near(0)
    share(1)
    take_far(0)
    take_far(1)
    more, total = near_sums(1)
    counts = counts + more
    sums[...] += total
    score_near(1)
    take_far(2)
    score_far((0, 1))
    score_far((2,))
    for g, (_, base, count) in enumerate(GROUPS):
        half = WIDTH[g] // 2
        pieces = []
        for h in range(-(-half // 128)):
            size = min(128, half - 128 * h)
            best = jnp.max(top[g, :, 128 * h:128 * h + size], axis=0, keepdims=True)
            pieces.append(jnp.broadcast_to(best, (128, size)).T)
        best = jnp.concatenate(pieces, axis=0)
        best = jnp.maximum(best, jnp.max(acc[g][...], axis=1, keepdims=True)) * (1.0 / D)
        for i in range(NXY // 2):
            column[i, base:base + count, :] = best[count * i:count * i + count, :]
    for kk in range(3):
        best = jnp.max(top_far[kk], axis=0, keepdims=True)
        if kk < 2:
            mine = jnp.broadcast_to(jnp.max(acc_far[kk], axis=1, keepdims=True), (ROOM // 2, 128))
            mine = jnp.concatenate([jnp.where(c == h, mine, -float(D)) for h in range(2)], axis=0)
            best = jnp.maximum(best, mine.T[0:1, :])
        far_out[kk, :, 0:128] = best * (1.0 / D)
        far_out[kk, :, 128:256] = over
    far_back = []
    for kk, k in enumerate(FAR):
        there = FAR.index(NZ - k)
        for core in range(2):
            far_back.append(send(
                far_out.at[kk], far_z.at[c, there], us.at[core, kk], ur.at[c, there], (at_z(k)[0], core)))
    for i in range(NXY // 2):
        best_out[i] = jnp.where(last, over, column[i].T[0:1, :])

    def best_copy(i, other):
        jx, jy = 2 * c + i // 4, i % 4
        there = (z * 16 + ((x + jx) % 4) * 4 + (y + jy) % 4, 1 - c if other else c)
        return pltpu.make_async_remote_copy(
            best_out.at[i], ret1.at[8 * c + i], bs.at[int(other), i], br.at[8 * c + i],
            device_id=there, device_id_type=MESH)

    @pl.when(c == 0)
    def _():
        ret1[0] = best_out[0]

    @pl.when(c == 1)
    def _():
        best_copy(0, False).start()

    best_copy(0, True).start()
    for i in range(1, 8):
        best_copy(i, False).start()
        best_copy(i, True).start()

    for kk in range(3):
        more, part = member_sums(ik_far[kk], z_far[kk])
        counts = counts + more
        total = part if kk == 0 else total + part
    cent_load.wait()
    mass_load.wait()
    number = jnp.sum(counts, axis=1, keepdims=True)
    mass = jnp.broadcast_to(mass_v[...], (128, CLUSTERS)).T[:, 0:1]
    cent[...] = (mass * cent[...] + (sums[...] + total)) / (mass + number)
    nc_copy = pltpu.make_async_copy(cent, nc_ref, local_sem.at[2])
    nc_copy.start()

    @pl.when(c == 1)
    def _():
        best_copy(0, False).wait_send()

    best_copy(0, True).wait_send()
    for i in range(1, 8):
        best_copy(i, False).wait_send()
        best_copy(i, True).wait_send()

    def best_arrived(j):
        pltpu.make_async_remote_copy(
            best_out.at[0], ret1.at[j], bs.at[0, 0], br.at[j], device_id=partner, device_id_type=MESH).wait_recv()

    @pl.when(c == 1)
    def _():
        best_arrived(0)

    for j in range(1, NXY):
        best_arrived(j)
    back = {}
    for k in (2, 6, 1, 7):
        back[NZ - k] = send(ret1, ret2.at[NZ - k], fs.at[k], fr.at[NZ - k], at_z(k))
    for h in range(2):
        for kk in range(3):
            pltpu.make_async_remote_copy(
                far_out.at[kk], far_z.at[h, kk], us.at[0, kk], ur.at[h, kk],
                device_id=partner, device_id_type=MESH).wait_recv()
    lane16 = lax.broadcasted_iota(jnp.int32, (NXY, 128), 1)
    got = jnp.zeros((NXY, 128), jnp.float32)
    for kk in range(3):
        line = jnp.maximum(far_z[0, kk][:, 0:128], far_z[1, kk][:, 0:128])
        line = jnp.broadcast_to(line, (8, 128))
        found = jnp.concatenate(
            [jnp.take_along_axis(line, back_at[8 * h:8 * h + 8, :], axis=1, mode="promise_in_bounds") for h in range(2)],
            axis=0)
        got = jnp.where(lane16 >= kk * CAP, found, got)
    far_over = far_z[0, 0][:, 128:256]
    for h in range(2):
        for kk in range(3):
            far_over = jnp.maximum(far_over, far_z[h, kk][:, 128:256])
    got = jnp.where(lane16 == 127, far_over, got)
    far_home = {}
    for j in range(NXY):
        if j == 0:
            far_ret[0] = got[0:1, :]
        else:
            back_out[j] = got[j:j + 1, :]
            far_home[neg(j)] = send(back_out.at[j], far_ret.at[neg(j)], ts.at[j], tr.at[neg(j)], at_xy(j))
    tile_t = tiles_i[0]
    lane_t = tiles_i[1]
    result = jnp.zeros((8, 128), jnp.float32)
    flag = jnp.zeros((1, 128), jnp.float32)

    def pick(line, tile, result, flag):
        got = jnp.take_along_axis(jnp.broadcast_to(line, (8, 128)), lane_t, axis=1, mode="promise_in_bounds")
        return jnp.where(tile_t == tile, got, result), jnp.maximum(flag, jnp.where(last, line, 0.0))

    for j in range(NXY):
        result, flag = pick(ret1[j], j, result, flag)
    for k in NEAR:
        back[k].wait_recv()
        for j in range(NXY):
            result, flag = pick(ret2[k, j], k * NXY + j, result, flag)
    for d in range(NXY):
        if d:
            far_home[d].wait_recv()
        result, flag = pick(far_ret[d], NZ * NXY + d, result, flag)
    for b in range(ROWS // 128):
        best_ref[:, 128 * b:128 * b + 128] = result[b:b + 1, :]
    flag_ref[0, 0] = jnp.max(flag).astype(jnp.int32)

    for group in (back, meta_copies, z_copies, x_copies, id_copies, p_copies, f_copies, fid_copies, far_home):
        for copy in group.values():
            copy.wait_send()
    for copy in far_back:
        copy.wait_send()
    nc_copy.wait()


def compact(embeddings, cluster_id, centroids, cluster_mass):
    vmem = pl.BlockSpec(memory_space=pltpu.VMEM)
    anywhere = pl.BlockSpec(memory_space=pl.ANY)
    f32, bf16, i32 = jnp.float32, jnp.bfloat16, jnp.int32
    dma = pltpu.SemaphoreType.DMA
    line = (1, 128)
    return pl.pallas_call(
        exchange_kernel,
        out_shape=(
            jax.ShapeDtypeStruct((1, ROWS), f32),
            jax.ShapeDtypeStruct((CLUSTERS, HALF), f32),
            jax.ShapeDtypeStruct((1, 1), i32),
        ),
        in_specs=[anywhere, anywhere, anywhere, anywhere],
        out_specs=(vmem, anywhere, pl.BlockSpec(memory_space=pltpu.SMEM)),
        scratch_shapes=[
            pltpu.VMEM((ROWS, HALF), f32),
            pltpu.VMEM((ROWS, HALF), bf16),
            pltpu.VMEM((1, ROWS), f32),
            pltpu.VMEM((1, ROWS), f32),
            pltpu.VMEM((NZ, ROOM, HALF), bf16),
            pltpu.VMEM((NZ, ROOM, HALF), bf16),
            pltpu.VMEM((3, ROOM, HALF), bf16),
            pltpu.VMEM((3, ROOM, HALF), bf16),
            pltpu.VMEM((NZ, 8, 128), f32),
            pltpu.VMEM((NZ, 8, 128), f32),
            *[pltpu.VMEM((NXY, count, HALF), bf16) for _, _, count in GROUPS],
            pltpu.VMEM((NXY, *line), f32),
            *[pltpu.VMEM((NXY, far[2], HALF), bf16) for far in FAR_SETS],
            *[pltpu.VMEM((NXY, far[2], HALF), bf16) for far in FAR_SETS],
            pltpu.VMEM((NXY, *line), f32),
            pltpu.VMEM((NXY, *line), f32),
            *[pltpu.VMEM((NXY, count, HALF), bf16) for _, _, count in GROUPS],
            *[pltpu.VMEM((NXY, count, HALF), bf16) for _, _, count in GROUPS],
            pltpu.VMEM((NXY, *line), f32),
            *[pltpu.VMEM((NXY * count, 128), f32) for _, _, count in GROUPS],
            pltpu.VMEM((3, 128, 128), f32),
            pltpu.VMEM((2, 8, 384), f32),
            pltpu.VMEM((2, 8, 384), f32),
            *[pltpu.VMEM((width // 2, 128), f32) for width in WIDTH],
            pltpu.VMEM((2, ROOM // 2, 128), f32),
            pltpu.VMEM((3, 8, 128), f32),
            pltpu.VMEM((CLUSTERS, HALF), f32),
            pltpu.VMEM((2, 8, 128), i32),
            pltpu.VMEM((8, 128, 128), f32),
            pltpu.VMEM((8, *line), f32),
            pltpu.VMEM((3, 1, 256), f32),
            pltpu.VMEM((NXY, *line), f32),
            pltpu.VMEM((NZ, NXY, *line), f32),
            pltpu.VMEM((2, 3, 1, 256), f32),
            pltpu.VMEM((NXY, *line), f32),
            pltpu.VMEM((NXY, *line), f32),
            pltpu.VMEM((CLUSTERS, HALF), f32),
            pltpu.VMEM((ROWS,), i32),
            pltpu.VMEM((1, CLUSTERS), f32),
            dma((5,)), dma((2,)), dma((NZ,)), dma((NZ,)), dma((NZ,)), dma((NZ,)),
            dma((2, NXY)), dma((2, NXY)), dma((NXY,)), dma((NXY,)), dma((5, NXY)), dma((5, NXY)),
            dma((2, 8)), dma((NXY,)), dma((NZ,)), dma((NZ,)),
            dma((2, NXY)), dma((2, NXY)), dma((NXY,)), dma((NXY,)), dma((2, 3)), dma((2, 3)), dma((NXY,)), dma((NXY,)),
        ],
        compiler_params=pltpu.CompilerParams(
            collective_id=0, has_side_effects=True, vmem_limit_bytes=48 * 2**20),
    )(embeddings, cluster_id, centroids, cluster_mass.reshape(1, CLUSTERS))


def from_partner(value):
    return lax.ppermute(value, "mp", [(0, 1), (1, 0)])


def general(embeddings, cluster_id, centroids, cluster_mass):
    owners = lax.axis_size("dp")
    row_count = embeddings.shape[0]
    slot_count = 2 * row_count
    capacity = slot_count // owners
    cluster_count = centroids.shape[0]
    core = lax.axis_index("mp")
    squares = jnp.sum(embeddings * embeddings, axis=1)
    squares = squares + from_partner(squares)
    unit = (embeddings * lax.rsqrt(squares / D + 1e-06)[:, None]).astype(jnp.bfloat16)
    owner = cluster_id // cluster_count
    local = cluster_id - owner * cluster_count
    owner_hot = (owner[:, None] == jnp.arange(owners, dtype=jnp.int32)[None, :]).astype(jnp.bfloat16)
    row_index = jnp.arange(row_count, dtype=jnp.int32)
    lower = (row_index[:, None] >= row_index[None, :]).astype(jnp.bfloat16)
    running = jnp.dot(lower, owner_hot, preferred_element_type=jnp.float32)
    rank = jnp.sum(running * owner_hot.astype(jnp.float32), axis=1).astype(jnp.int32) - 1
    slot = owner * capacity + rank
    slot_index = jnp.arange(slot_count, dtype=jnp.int32)
    placed = slot_index[:, None] == slot[None, :]
    outgoing = jnp.dot(
        placed.astype(jnp.bfloat16), unit, preferred_element_type=jnp.float32
    ).astype(jnp.bfloat16)
    out_ids = jnp.max(jnp.where(placed, local[None, :] + 1, 0), axis=1) - 1
    incoming = lax.all_to_all(outgoing, "dp", split_axis=0, concat_axis=0, tiled=True)
    in_ids = lax.all_to_all(out_ids, "dp", split_axis=0, concat_axis=0, tiled=True)
    member = (jnp.arange(cluster_count, dtype=jnp.int32)[:, None] == in_ids[None, :]).astype(jnp.bfloat16)
    sums = jnp.dot(member, incoming, preferred_element_type=jnp.float32)
    counts = jnp.sum(member.astype(jnp.float32), axis=1)
    new_centroids = (cluster_mass[:, None] * centroids + sums) / (cluster_mass + counts)[:, None]
    half = slot_count // 2
    start = core * half
    contract = (((1,), (1,)), ((), ()))
    other = from_partner(incoming)
    scores = lax.dot_general(
        lax.dynamic_slice_in_dim(incoming, start, half, 0), incoming, contract, preferred_element_type=jnp.float32)
    scores = scores + lax.dot_general(
        lax.dynamic_slice_in_dim(other, start, half, 0), other, contract, preferred_element_type=jnp.float32)
    scores = scores / D
    query_ids = lax.dynamic_slice_in_dim(in_ids, start, half, 0)
    query_pos = start + jnp.arange(half, dtype=jnp.int32)
    same = (
        (query_ids[:, None] == in_ids[None, :])
        & (query_ids[:, None] >= 0)
        & (query_pos[:, None] != slot_index[None, :])
    )
    best = jnp.max(jnp.where(same, scores, -1.0), axis=1)
    best_p = from_partner(best)
    low, high = jnp.where(core == 0, best, best_p), jnp.where(core == 0, best_p, best)
    returned = lax.all_to_all(
        jnp.concatenate([low, high]), "dp", split_axis=0, concat_axis=0, tiled=True)
    return jnp.take(returned, slot), new_centroids


def shards(embeddings, cluster_id, centroids, cluster_mass):
    best, new_centroids, flag = compact(embeddings, cluster_id, centroids, cluster_mass)
    return lax.cond(
        flag[0, 0] > 0,
        lambda *args: general(*args),
        lambda *args: (best.reshape(ROWS), new_centroids),
        embeddings, cluster_id, centroids, cluster_mass,
    )


def solution(mesh):
    in_specs = (P("dp", "mp"), P("dp"), P("dp", "mp"), P("dp"))
    out_specs = (P("dp"), P("dp", "mp"))
    return jax.shard_map(shards, mesh=mesh, in_specs=in_specs, out_specs=out_specs, check_vma=False)
```

time: 67.8 us -> 58.4 us (0.86)
  Pallas kernels: 63.7 us -> 55.8 us
  local copies, waits for them, and re-layouts: 2.24 us -> 0.82 us
    pallas_call x1, Pallas kernels: 63.7 us -> 55.8 us  [compact(): pl.pallas_call(exchange_kernel, out_shape=(jax.ShapeDtypeStruct((1, ROWS)...]
    reshape x1 -> x0, local copies, waits for them, and re-layouts: 0.83 us -> none  [compact(): cluster_id.reshape(1, ROWS)]
where the time goes in v3:
time: 58.4 us; the launch traced here: 58.3 us
  Pallas kernels  55.8 us (96%)
  between operations  1.41 us (2%)
  local copies, waits for them, and re-layouts  0.82 us (1%)
    pallas_call x1, Pallas kernels, compact(): pl.pallas_call(exchange_kernel, out_shape=(jax.ShapeDtypeStruct((1, ROWS)...  55.8 us

profile of v3, /device:TPU:1, one launch (start us, length us, event | category | flops | bytes accessed | tf_op | source)
XLA Modules:
  0.0 58.3 jit_solution(28700626912325372)
XLA Ops:
  0.6 0.0 copy-start
  0.6 0.0 copy-start.2
  0.7 0.0 copy-start.1
  0.7 0.0 copy-start.3
  0.7 55.8 %shard_map.61 = (f32[1,768]{1,0:T(1,128)S(1)}, f32[256,512]{1,0:T(8,128)S(1)}, s32[1,1]{1,0:T(1,128)}) custom-call(f32[768,512]{1,0:T(8,128)} %emb_ref.1, s32[768]{0:T(1024)} %cid_ref.1, f32[256,512]{1,0:T(8,128)} %cent_ref.1, f32[1,256]{1,0:T(1,128)} %bitcast.9), custom_call_target="tpu_custom_call" | custom-call | tf_op jit(solution)/shard_map/pallas_call | solution.py:586
  57.1 0.0 copy-done
  57.2 0.0 copy-done.2
  57.2 0.0 copy-done.1
  57.2 0.0 copy-done.3
  57.2 0.3 conditional.1
  57.4 0.0 copy-start.4
  57.5 0.8 %copy.19 = f32[256,512]{1,0:T(8,128)} copy(f32[256,512]{1,0:T(8,128)S(1)} %get-tuple-element.41) | data formatting | bytes 1048576
  58.3 0.0 copy-done.4
  (1 shorter events, 0.0 us)
Async XLA Ops:
  0.6 56.5 %copy-start = (f32[768,512]{1,0:T(8,128)S(1)}, f32[768,512]{1,0:T(8,128)}, u32[]{:S(2)}) copy-start(f32[768,512]{1,0:T(8,128)} %emb_ref.1) | copy-start | bytes 4718596
  0.6 56.5 %copy-start.2 = (s32[768]{0:T(1024)S(1)}, s32[768]{0:T(1024)}, u32[]{:S(2)}) copy-start(s32[768]{0:T(1024)} %cid_ref.1) | copy-start | bytes 9220
  0.7 56.5 %copy-start.1 = (f32[256,512]{1,0:T(8,128)S(1)}, f32[256,512]{1,0:T(8,128)}, u32[]{:S(2)}) copy-start(f32[256,512]{1,0:T(8,128)} %cent_ref.1) | copy-start | bytes 1572868
  0.7 56.5 %copy-start.3 = (f32[256]{0:T(256)S(1)}, f32[256]{0:T(256)}, u32[]{:S(2)}) copy-start(f32[256]{0:T(256)} %param.9) | copy-start | bytes 3076
  57.4 0.8 %copy-start.4 = (f32[768]{0:T(1024)}, f32[768]{0:T(1024)S(1)}, u32[]{:S(2)}) copy-start(f32[768]{0:T(1024)S(1)} %get-tuple-element.40) | copy-start | bytes 9220

commit v4 on v3

--- a/solution.py
+++ b/solution.py
@@ -23,6 +23,7 @@
 MESH = pl.DeviceIdType.MESH
 NT = (((1,), (1,)), ((), ()))
 NEAR = (1, 7, 2, 6)
+POS = {k: i for i, k in enumerate((0,) + NEAR + FAR)}
 
 
 def neg(d):
@@ -60,6 +61,14 @@
         copy = pltpu.make_async_remote_copy(src, dst, send_sem, recv_sem, device_id=to, device_id_type=MESH)
         copy.start()
         return copy
+
+    def sent(ref, sem):
+        pltpu.make_async_remote_copy(ref, ref, sem, sem, device_id=partner, device_id_type=MESH).wait_send()
+
+    def arrived(ref, sem):
+        pltpu.make_async_remote_copy(ref, ref, sem, sem, device_id=partner, device_id_type=MESH).wait_recv()
+
+    others = pl.ds(1, NXY - 1)
 
     cid_load = pltpu.make_async_copy(cid_ref, cid_v, local_sem.at[3])
     cid_load.start()
@@ -159,15 +168,13 @@
     for f in range(HALF // 128):
         unit[:, 128 * f:128 * f + 128] = (emb[:, 128 * f:128 * f + 128] * scale).astype(jnp.bfloat16)
 
-    z_copies, meta_copies, f_copies, fid_copies = {}, {}, {}, {}
-
     def pack(k):
         packed = jnp.dot(place_hot[k], unit[...], preferred_element_type=jnp.float32).astype(jnp.bfloat16)
         if k == 0:
             zin[0] = packed
         else:
-            zout[k] = packed
-            z_copies[NZ - k] = send(zout.at[k], zin.at[NZ - k], zs.at[k], zr.at[NZ - k], at_z(k))
+            zout[POS[k]] = packed
+            send(zout.at[POS[k]], zin.at[POS[NZ - k]], zs.at[0], zr.at[0 if k in (1, 7) else 1], at_z(k))
 
     pack(1)
     pack(7)
@@ -180,7 +187,7 @@
             fid_in[0] = ids[0:1, :]
         else:
             fid_out[d] = ids[d:d + 1, :]
-            fid_copies[neg(d)] = send(fid_out.at[d], fid_in.at[neg(d)], vs.at[d], vr.at[neg(d)], at_xy(d))
+            send(fid_out.at[d], fid_in.at[neg(d)], vs.at[0], vr.at[0], at_xy(d))
 
     def pack_far(e):
         count = FAR_SETS[e][2]
@@ -191,8 +198,7 @@
                 fin[e][0] = block
             else:
                 fout[e][d] = block
-                f_copies[e, neg(d)] = send(
-                    fout[e].at[d], fin[e].at[neg(d)], ws.at[e, d], wr.at[e, neg(d)], at_xy(d))
+                send(fout[e].at[d], fin[e].at[neg(d)], ws.at[e], wr.at[e], at_xy(d))
 
     pack_far(0)
     pack_far(1)
@@ -201,28 +207,28 @@
         if k == 0:
             min_[0] = meta
         else:
-            mout[k] = meta
-            meta_copies[NZ - k] = send(mout.at[k], min_.at[NZ - k], ms.at[k], mr.at[NZ - k], at_z(k))
+            mout[POS[k]] = meta
+            send(mout.at[POS[k]], min_.at[POS[NZ - k]], ms.at[0], mr.at[0 if k in (1, 7) else 1], at_z(k))
     pack(2)
     pack(6)
     pack(0)
 
-    x_copies, p_copies = {}, {}
+    p_copies = {}
 
     def forward(g):
         members, _, count = GROUPS[g]
         total = None
+        if g == 0:
+            arrived(min_.at[pl.ds(1, 2)], mr.at[0])
         for m, k in enumerate(members):
-            if g == 0 and k:
-                meta_copies[k].wait_recv()
-            meta = min_[k]
+            meta = min_[POS[k]]
             valid = meta[0:1, :] > 0.5
             there = jnp.where(valid, meta[1:2, :] * float(count) + meta[2:3, :] + float(CAP * m), -1.0)
             there = there.astype(jnp.int32)
             want = lax.broadcasted_iota(jnp.int32, (NXY * count, ROOM), 0)
-            if k:
-                z_copies[k].wait_recv()
-            part = jnp.dot(hot(want == there), zin[k], preferred_element_type=jnp.float32)
+            if m == g ^ 1:
+                arrived(zin.at[pl.ds(1 + 2 * g, 2)], zr.at[g])
+            part = jnp.dot(hot(want == there), zin[POS[k]], preferred_element_type=jnp.float32)
             total = part if total is None else total + part
         for d in range(NXY):
             block = total[count * d:count * d + count, :].astype(jnp.bfloat16)
@@ -230,21 +236,17 @@
                 rows[g][0] = block
             else:
                 xout[g][d] = block
-                x_copies[g, neg(d)] = send(
-                    xout[g].at[d], rows[g].at[neg(d)], xs.at[g, d], xr.at[g, neg(d)], at_xy(d))
+                send(xout[g].at[d], rows[g].at[neg(d)], xs.at[g], xr.at[g], at_xy(d))
 
     def share(g):
-        for j in range(NXY):
-            if j:
-                x_copies[g, j].wait_recv()
-            p_copies[g, j] = send(rows[g].at[j], rows_p[g].at[j], ps.at[g, j], pr.at[g, j], partner)
+        arrived(rows[g].at[others], xr.at[g])
+        p_copies[g] = send(rows[g], rows_p[g], ps.at[g], pr.at[g], partner)
 
     def share_far(kk):
-        z_copies[FAR[kk]].wait_recv()
-        p_copies[2 + kk, 0] = send(z_far.at[kk], z_far_p.at[kk], ps.at[2 + kk, 0], pr.at[2 + kk, 0], partner)
-
-    for j in range(1, NXY):
-        fid_copies[j].wait_recv()
+        arrived(z_far.at[kk], zr.at[2 + kk])
+        p_copies[2 + kk] = send(z_far.at[kk], z_far_p.at[kk], ps.at[2 + kk], pr.at[2 + kk], partner)
+
+    arrived(fid_in.at[others], vr.at[0])
     known = jnp.concatenate([fid_in[j] for j in range(NXY)], axis=0).astype(jnp.bfloat16)
     back_at = jnp.zeros((NXY, 128), jnp.float32)
     far_values, far_places = [], []
@@ -283,43 +285,40 @@
         for m, k in enumerate(planes):
             want = lax.broadcasted_iota(jnp.int32, (ROOM, width), 0).astype(jnp.float32)
             chosen.append(hot(want == far_places[e][m:m + 1, :]))
-            mout[k] = lax.dot_general(far_values[e], chosen[m], NT, preferred_element_type=jnp.float32)
-            meta_copies[NZ - k] = send(mout.at[k], min_.at[NZ - k], ms.at[k], mr.at[NZ - k], at_z(k))
-        for j in range(1, NXY):
-            f_copies[e, j].wait_recv()
+            mout[POS[k]] = lax.dot_general(far_values[e], chosen[m], NT, preferred_element_type=jnp.float32)
+            there = FAR.index(NZ - k)
+            send(mout.at[POS[k]], min_.at[POS[NZ - k]], ms.at[0], mr.at[2 + there], at_z(k))
+        arrived(fin[e].at[others], wr.at[e])
         for m, k in enumerate(planes):
-            zout[k] = jnp.dot(
+            zout[POS[k]] = jnp.dot(
                 chosen[m], fin[e][...].reshape(width, HALF), preferred_element_type=jnp.float32).astype(jnp.bfloat16)
-            z_copies[NZ - k] = send(
-                zout.at[k], z_far.at[FAR.index(NZ - k)], zs.at[k], zr.at[NZ - k], at_z(k))
+            there = FAR.index(NZ - k)
+            send(zout.at[POS[k]], z_far.at[there], zs.at[0], zr.at[2 + there], at_z(k))
 
     forward(0)
     relay_far(0)
 
-    for k in (2, 6):
-        meta_copies[k].wait_recv()
+    arrived(min_.at[pl.ds(3, 2)], mr.at[1])
     ids = jnp.zeros((NXY, 128), jnp.float32)
     for k in (0,) + NEAR:
-        meta = min_[k]
+        meta = min_[POS[k]]
         valid = meta[0:1, :] > 0.5
         to = jnp.where(valid, meta[1:2, :], -1.0).astype(jnp.int32)
         place_k = meta[2:3, :].astype(jnp.int32) + LANE[k]
         left = jnp.where(sub16 == to, meta[0:1, :], 0.0).astype(jnp.bfloat16)
         ids = ids + lax.dot_general(left, hot(sub128 == place_k), NT, preferred_element_type=jnp.float32)
-    id_copies = {}
     for d in range(NXY):
         if d == 0:
             idin[0] = ids[0:1, :]
         else:
             idout[d] = ids[d:d + 1, :]
-            id_copies[neg(d)] = send(idout.at[d], idin.at[neg(d)], ids_s.at[d], ids_r.at[neg(d)], at_xy(d))
+            send(idout.at[d], idin.at[neg(d)], ids_s.at[0], ids_r.at[0], at_xy(d))
 
     forward(1)
     relay_far(1)
 
     share(0)
-    for j in range(1, NXY):
-        id_copies[j].wait_recv()
+    arrived(idin.at[others], ids_r.at[0])
     for j in range(NXY):
         line = idin[j]
         line = jnp.where(line < 0.5, -1.0, line)
@@ -365,8 +364,7 @@
     def score_near(e):
         pairs = [(e, e)] + [pair for g in range(e) for pair in ((g, e), (e, g))]
         own = [nt(keys_of(kg)[0], own_half(qg)[0]) for kg, qg in pairs]
-        for j in range(NXY):
-            p_copies[e, j].wait_recv()
+        p_copies[e].wait_recv()
         for (kg, qg), part in zip(pairs, own):
             nk, nq = WIDTH[kg], WIDTH[qg] // 2
             scores = part + nt(keys_of(kg)[1], own_half(qg)[1])
@@ -396,7 +394,7 @@
         columns = z_far[cut].reshape(width, HALF)
         own = [nt(side(g)[0], columns) for g in groups]
         for kk in planes:
-            p_copies[2 + kk, 0].wait_recv()
+            p_copies[2 + kk].wait_recv()
         columns = z_far_p[cut].reshape(width, HALF)
         for g, part in zip(groups, own):
             scores = part + nt(side(g)[1], columns)
@@ -406,7 +404,7 @@
             else:
                 mine = ik_far[g - 2, half_far, :]
             for kk in planes:
-                line = min_[FAR[kk]][0:1, :]
+                line = min_[POS[FAR[kk]]][0:1, :]
                 same = mine == line
                 if g == 2 + kk:
                     apart = (lax.broadcasted_iota(jnp.int32, (n, ROOM), 1)
@@ -420,8 +418,8 @@
                     acc_far[g - 2] = jnp.maximum(acc_far[g - 2], kept)
 
     def take_far(kk):
-        meta_copies[FAR[kk]].wait_recv()
-        line = min_[FAR[kk]][0:1, :]
+        arrived(min_.at[POS[FAR[kk]]], mr.at[2 + kk])
+        line = min_[POS[FAR[kk]]][0:1, :]
         ik_far[kk] = jnp.broadcast_to(jnp.where(line < 0.5, -1.0, line), (128, 128)).T
         share_far(kk)
 
@@ -435,8 +433,8 @@
     counts = counts + more
     sums[...] += total
     score_near(1)
+    score_far((0, 1))
     take_far(2)
-    score_far((0, 1))
     score_far((2,))
     for g, (_, base, count) in enumerate(GROUPS):
         half = WIDTH[g] // 2
@@ -457,12 +455,10 @@
             best = jnp.maximum(best, mine.T[0:1, :])
         far_out[kk, :, 0:128] = best * (1.0 / D)
         far_out[kk, :, 128:256] = over
-    far_back = []
     for kk, k in enumerate(FAR):
         there = FAR.index(NZ - k)
         for core in range(2):
-            far_back.append(send(
-                far_out.at[kk], far_z.at[c, there], us.at[core, kk], ur.at[c, there], (at_z(k)[0], core)))
+            send(far_out.at[kk], far_z.at[c, there], us.at[core], ur.at[0], (at_z(k)[0], core))
     for i in range(NXY // 2):
         best_out[i] = jnp.where(last, over, column[i].T[0:1, :])
 
@@ -470,7 +466,7 @@
         jx, jy = 2 * c + i // 4, i % 4
         there = (z * 16 + ((x + jx) % 4) * 4 + (y + jy) % 4, 1 - c if other else c)
         return pltpu.make_async_remote_copy(
-            best_out.at[i], ret1.at[8 * c + i], bs.at[int(other), i], br.at[8 * c + i],
+            best_out.at[i], ret1.at[8 * c + i], bs.at[int(other)], br.at[0],
             device_id=there, device_id_type=MESH)
 
     @pl.when(c == 0)
@@ -498,33 +494,19 @@
     nc_copy = pltpu.make_async_copy(cent, nc_ref, local_sem.at[2])
     nc_copy.start()
 
+    @pl.when(c == 0)
+    def _():
+        arrived(ret1.at[others], br.at[0])
+
     @pl.when(c == 1)
     def _():
-        best_copy(0, False).wait_send()
-
-    best_copy(0, True).wait_send()
-    for i in range(1, 8):
-        best_copy(i, False).wait_send()
-        best_copy(i, True).wait_send()
-
-    def best_arrived(j):
-        pltpu.make_async_remote_copy(
-            best_out.at[0], ret1.at[j], bs.at[0, 0], br.at[j], device_id=partner, device_id_type=MESH).wait_recv()
-
-    @pl.when(c == 1)
-    def _():
-        best_arrived(0)
-
-    for j in range(1, NXY):
-        best_arrived(j)
+        arrived(ret1, br.at[0])
+
     back = {}
     for k in (2, 6, 1, 7):
-        back[NZ - k] = send(ret1, ret2.at[NZ - k], fs.at[k], fr.at[NZ - k], at_z(k))
-    for h in range(2):
-        for kk in range(3):
-            pltpu.make_async_remote_copy(
-                far_out.at[kk], far_z.at[h, kk], us.at[0, kk], ur.at[h, kk],
-                device_id=partner, device_id_type=MESH).wait_recv()
+        back[NZ - k] = send(
+            ret1, ret2.at[POS[NZ - k] - 1], fs.at[POS[k] - 1], fr.at[POS[NZ - k] - 1], at_z(k))
+    arrived(far_z, ur.at[0])
     lane16 = lax.broadcasted_iota(jnp.int32, (NXY, 128), 1)
     got = jnp.zeros((NXY, 128), jnp.float32)
     for kk in range(3):
@@ -539,13 +521,12 @@
         for kk in range(3):
             far_over = jnp.maximum(far_over, far_z[h, kk][:, 128:256])
     got = jnp.where(lane16 == 127, far_over, got)
-    far_home = {}
     for j in range(NXY):
         if j == 0:
             far_ret[0] = got[0:1, :]
         else:
             back_out[j] = got[j:j + 1, :]
-            far_home[neg(j)] = send(back_out.at[j], far_ret.at[neg(j)], ts.at[j], tr.at[neg(j)], at_xy(j))
+            send(back_out.at[j], far_ret.at[neg(j)], ts.at[0], tr.at[0], at_xy(j))
     tile_t = tiles_i[0]
     lane_t = tiles_i[1]
     result = jnp.zeros((8, 128), jnp.float32)
@@ -560,20 +541,34 @@
     for k in NEAR:
         back[k].wait_recv()
         for j in range(NXY):
-            result, flag = pick(ret2[k, j], k * NXY + j, result, flag)
+            result, flag = pick(ret2[POS[k] - 1, j], k * NXY + j, result, flag)
+    arrived(far_ret.at[others], tr.at[0])
     for d in range(NXY):
-        if d:
-            far_home[d].wait_recv()
         result, flag = pick(far_ret[d], NZ * NXY + d, result, flag)
     for b in range(ROWS // 128):
         best_ref[:, 128 * b:128 * b + 128] = result[b:b + 1, :]
     flag_ref[0, 0] = jnp.max(flag).astype(jnp.int32)
 
-    for group in (back, meta_copies, z_copies, x_copies, id_copies, p_copies, f_copies, fid_copies, far_home):
-        for copy in group.values():
-            copy.wait_send()
-    for copy in far_back:
+    @pl.when(c == 0)
+    def _():
+        sent(best_out.at[pl.ds(1, 7)], bs.at[0])
+
+    @pl.when(c == 1)
+    def _():
+        sent(best_out, bs.at[0])
+
+    sent(best_out, bs.at[1])
+    for copy in list(back.values()) + list(p_copies.values()):
         copy.wait_send()
+    sent(zout.at[pl.ds(1, NZ - 1)], zs.at[0])
+    sent(mout.at[pl.ds(1, NZ - 1)], ms.at[0])
+    for e in range(2):
+        sent(xout[e].at[others], xs.at[e])
+        sent(fout[e].at[others], ws.at[e])
+        sent(far_out, us.at[e])
+    sent(fid_out.at[others], vs.at[0])
+    sent(idout.at[others], ids_s.at[0])
+    sent(back_out.at[others], ts.at[0])
     nc_copy.wait()
 
 
@@ -598,7 +593,7 @@
             pltpu.VMEM((1, ROWS), f32),
             pltpu.VMEM((1, ROWS), f32),
             pltpu.VMEM((NZ, ROOM, HALF), bf16),
-            pltpu.VMEM((NZ, ROOM, HALF), bf16),
+            pltpu.VMEM((1 + len(NEAR), ROOM, HALF), bf16),
             pltpu.VMEM((3, ROOM, HALF), bf16),
             pltpu.VMEM((3, ROOM, HALF), bf16),
             pltpu.VMEM((NZ, 8, 128), f32),
@@ -625,17 +620,16 @@
             pltpu.VMEM((8, *line), f32),
             pltpu.VMEM((3, 1, 256), f32),
             pltpu.VMEM((NXY, *line), f32),
-            pltpu.VMEM((NZ, NXY, *line), f32),
+            pltpu.VMEM((len(NEAR), NXY, *line), f32),
             pltpu.VMEM((2, 3, 1, 256), f32),
             pltpu.VMEM((NXY, *line), f32),
             pltpu.VMEM((NXY, *line), f32),
             pltpu.VMEM((CLUSTERS, HALF), f32),
             pltpu.VMEM((ROWS,), i32),
             pltpu.VMEM((1, CLUSTERS), f32),
-            dma((5,)), dma((2,)), dma((NZ,)), dma((NZ,)), dma((NZ,)), dma((NZ,)),
-            dma((2, NXY)), dma((2, NXY)), dma((NXY,)), dma((NXY,)), dma((5, NXY)), dma((5, NXY)),
-            dma((2, 8)), dma((NXY,)), dma((NZ,)), dma((NZ,)),
-            dma((2, NXY)), dma((2, NXY)), dma((NXY,)), dma((NXY,)), dma((2, 3)), dma((2, 3)), dma((NXY,)), dma((NXY,)),
+            dma((5,)), dma((2,)), dma((1,)), dma((5,)), dma((1,)), dma((5,)), dma((2,)), dma((2,)),
+            dma((1,)), dma((1,)), dma((5,)), dma((5,)), dma((2,)), dma((1,)), dma((4,)), dma((4,)),
+            dma((2,)), dma((2,)), dma((1,)), dma((1,)), dma((2,)), dma((1,)), dma((1,)), dma((1,)),
         ],
         compiler_params=pltpu.CompilerParams(
             collective_id=0, has_side_effects=True, vmem_limit_bytes=48 * 2**20),

time: 58.4 us -> 54 us (0.925)
  Pallas kernels: 55.8 us -> 51.5 us
    pallas_call x1, Pallas kernels: 55.8 us -> 51.5 us  [compact(): pl.pallas_call(exchange_kernel, out_shape=(jax.ShapeDtypeStruct((1, ROWS)...]
where the time goes in v4:
time: 54 us; the launch traced here: 53.9 us
  Pallas kernels  51.5 us (95%)
  between operations  1.41 us (3%)
  local copies, waits for them, and re-layouts  0.82 us (2%)
    pallas_call x1, Pallas kernels, compact(): pl.pallas_call(exchange_kernel, out_shape=(jax.ShapeDtypeStruct((1, ROWS)...  51.5 us

profile of v4, /device:TPU:1, one launch (start us, length us, event | category | flops | bytes accessed | tf_op | source)
XLA Modules:
  0.0 53.9 jit_solution(913429924827165602)
XLA Ops:
  0.6 0.0 copy-start
  0.6 0.0 copy-start.2
  0.7 0.0 copy-start.1
  0.7 0.0 copy-start.3
  0.7 51.5 %shard_map.61 = (f32[1,768]{1,0:T(1,128)S(1)}, f32[256,512]{1,0:T(8,128)S(1)}, s32[1,1]{1,0:T(1,128)}) custom-call(f32[768,512]{1,0:T(8,128)} %emb_ref.1, s32[768]{0:T(1024)} %cid_ref.1, f32[256,512]{1,0:T(8,128)} %cent_ref.1, f32[1,256]{1,0:T(1,128)} %bitcast.9), custom_call_target="tpu_custom_call" | custom-call | tf_op jit(solution)/shard_map/pallas_call | solution.py:581
  52.8 0.0 copy-done
  52.8 0.0 copy-done.2
  52.8 0.0 copy-done.1
  52.9 0.0 copy-done.3
  52.9 0.3 conditional.1
  53.1 0.0 copy-start.4
  53.1 0.8 %copy.19 = f32[256,512]{1,0:T(8,128)} copy(f32[256,512]{1,0:T(8,128)S(1)} %get-tuple-element.41) | data formatting | bytes 1048576
  53.9 0.0 copy-done.4
  (1 shorter events, 0.0 us)
Async XLA Ops:
  0.6 52.2 %copy-start = (f32[768,512]{1,0:T(8,128)S(1)}, f32[768,512]{1,0:T(8,128)}, u32[]{:S(2)}) copy-start(f32[768,512]{1,0:T(8,128)} %emb_ref.1) | copy-start | bytes 4718596
  0.6 52.2 %copy-start.2 = (s32[768]{0:T(1024)S(1)}, s32[768]{0:T(1024)}, u32[]{:S(2)}) copy-start(s32[768]{0:T(1024)} %cid_ref.1) | copy-start | bytes 9220
  0.7 52.2 %copy-start.1 = (f32[256,512]{1,0:T(8,128)S(1)}, f32[256,512]{1,0:T(8,128)}, u32[]{:S(2)}) copy-start(f32[256,512]{1,0:T(8,128)} %cent_ref.1) | copy-start | bytes 1572868
  0.7 52.2 %copy-start.3 = (f32[256]{0:T(256)S(1)}, f32[256]{0:T(256)}, u32[]{:S(2)}) copy-start(f32[256]{0:T(256)} %param.9) | copy-start | bytes 3076
  53.1 0.8 %copy-start.4 = (f32[768]{0:T(1024)}, f32[768]{0:T(1024)S(1)}, u32[]{:S(2)}) copy-start(f32[768]{0:T(1024)S(1)} %get-tuple-element.40) | copy-start | bytes 9220

commit v5 on v4

--- a/solution.py
+++ b/solution.py
@@ -15,15 +15,17 @@
 ROOM = 128
 NZ = 8
 NXY = 16
-GROUPS = (((0, 1, 7), 0, 40), ((2, 6), 40, 24))
-LANE = {k: base + CAP * m for members, base, _ in GROUPS for m, k in enumerate(members)}
+GROUPS = (((1, 7), 0, 24), ((2, 6), 24, 24), ((None, 0), 48, 24))
+LANE = {k: base + CAP * m for members, base, _ in GROUPS for m, k in enumerate(members) if k is not None}
+OWN = 2
 FAR = (3, 5, 4)
-FAR_SETS = (((3, 5), 0, 24, 2731, 16), ((4,), 2, 16, 1, 4))
+FAR_SETS = (((3, 5), 0, 24), ((4,), 2, 24))
 WIDTH = tuple(count * NXY for _, _, count in GROUPS)
 MESH = pl.DeviceIdType.MESH
 NT = (((1,), (1,)), ((), ()))
 NEAR = (1, 7, 2, 6)
-POS = {k: i for i, k in enumerate((0,) + NEAR + FAR)}
+AROUND = (10, 9, 11, 6, 14, 2, 8, 5, 7, 13, 15, 1, 3, 4, 12, 0)
+POS = {k: i for i, k in enumerate(NEAR + FAR)}
 
 
 def neg(d):
@@ -37,14 +39,14 @@
 def exchange_kernel(
     emb_ref, cid_ref, cent_ref, mass_ref,
     best_ref, nc_ref, flag_ref,
-    emb, unit, sq_mine, sq_peer, zout, zin, z_far, z_far_p, mout, min_, xo0, xo1, idout, fo0, fo1, fi0, fi1, fid_out, fid_in,
-    r0, r1, p0, p1, idin, ik0, ik1, ik_far, top, idq, acc0, acc1, acc_far, top_far, sums,
+    emb, unit, sq_mine, sq_peer, zout, zin, z_far, z_far_p, mout, min_, xo0, xo1, idout, fo0, fo1, fi0, fi1, fi1_p, fid_out, fid_in,
+    r0, r1, p0, p1, idin, ik0, ik1, ik2, ik_far, top, idq, acc0, acc1, acc2, acc_far, top_far, sums,
     tiles_i, column, best_out, far_out, ret1, ret2, far_z, back_out, far_ret, cent, cid_v, mass_v,
     local_sem, sq_sem, zs, zr, ms, mr, xs, xr, ids_s, ids_r, ps, pr, bs, br, fs, fr,
     ws, wr, vs, vr, us, ur, ts, tr,
 ):
-    xout, rows, rows_p, idkey = (xo0, xo1), (r0, r1), (p0, p1), (ik0, ik1)
-    fout, fin, acc = (fo0, fo1), (fi0, fi1), (acc0, acc1)
+    xout, rows, rows_p, idkey = (xo0, xo1), (r0, r1, fi1), (p0, p1, fi1_p), (ik0, ik1, ik2)
+    fout, fin, acc = (fo0, fo1), (fi0, fi1), (acc0, acc1, acc2)
     me = lax.axis_index("dp")
     c = lax.axis_index("mp")
     z, x, y = me // 16, (me // 4) % 4, me % 4
@@ -79,13 +81,14 @@
     cent_load = pltpu.make_async_copy(cent_ref, cent, local_sem.at[1])
     cent_load.start()
     barrier = pltpu.get_barrier_semaphore()
-    for k in range(1, NZ):
+    for k in FAR[::-1]:
         pl.semaphore_signal(barrier, inc=1, device_id=at_z(k), device_id_type=MESH)
-    for d in range(1, NXY):
+        pl.semaphore_signal(barrier, inc=1, device_id=(at_z(k)[0], 1 - c), device_id_type=MESH)
+    for d in AROUND[:-1]:
         pl.semaphore_signal(barrier, inc=1, device_id=at_xy(d), device_id_type=MESH)
         pl.semaphore_signal(barrier, inc=1, device_id=(at_xy(d)[0], 1 - c), device_id_type=MESH)
-    for k in FAR:
-        pl.semaphore_signal(barrier, inc=1, device_id=(at_z(k)[0], 1 - c), device_id_type=MESH)
+    for k in NEAR:
+        pl.semaphore_signal(barrier, inc=1, device_id=at_z(k), device_id_type=MESH)
     pl.semaphore_signal(barrier, inc=1, device_id=partner, device_id_type=MESH)
 
     cid_load.wait()
@@ -113,7 +116,7 @@
         places.append(jnp.sum(jnp.where(is_z, run_z, 0.0), axis=0, keepdims=True) - 1.0)
         base_t = jnp.broadcast_to(run_t[:, 127:128], (128, 128))
         base_z = jnp.broadcast_to(run_z[:, 127:128], (8, 128))
-    near_most = jnp.where((sub8 < 3) | (sub8 > 5), base_z, 0.0)
+    near_most = jnp.where((sub8 == 1) | (sub8 == 2) | (sub8 > 5), base_z, 0.0)
     over = jnp.where(jnp.max(near_most, axis=0, keepdims=True) > float(ROOM), 1.0, 0.0)
     rank_f = jnp.concatenate(ranks, axis=1)
     rank = rank_f.astype(jnp.int32)
@@ -121,10 +124,10 @@
     slot = jnp.where(place < ROOM, dz * ROOM + place, -1)
     far_row = (dz >= 3) & (dz <= 5)
     far_lane = jnp.where(dz == 3, rank, jnp.where(dz == 5, rank + CAP, rank + 2 * CAP))
-    far_lane = jnp.where(far_row, far_lane, -1)
+    far_lane = jnp.where(far_row, far_lane, jnp.where(dz == 0, rank + 3 * CAP, -1))
     far_slot = (
         jnp.where((dz == 3) | (dz == 5), dxy * FAR_SETS[0][2] + far_lane, -1),
-        jnp.where(dz == 4, dxy * FAR_SETS[1][2] + rank, -1),
+        jnp.where((dz == 4) | (dz == 0), dxy * FAR_SETS[1][2] + far_lane - 2 * CAP, -1),
     )
     turned = ((4 - (dxy >> 2)) & 3) * 4 + ((4 - (dxy & 3)) & 3)
     tile_of = jnp.where(far_row, NZ * NXY + dxy, dz * NXY + turned)
@@ -154,12 +157,12 @@
     sq_copy = send(sq_mine, sq_peer, sq_sem.at[0], sq_sem.at[1], partner)
 
     place_hot = {}
-    for k in (0,) + NEAR:
+    for k in NEAR:
         want = lax.broadcasted_iota(jnp.int32, (ROOM, ROWS), 0) + k * ROOM
         place_hot[k] = hot(want == slot)
     far_hot = [
         hot(lax.broadcasted_iota(jnp.int32, (NXY * count, ROWS), 0) == far_slot[e])
-        for e, (_, _, count, _, _) in enumerate(FAR_SETS)
+        for e, (_, _, count) in enumerate(FAR_SETS)
     ]
 
     sq_copy.wait()
@@ -170,19 +173,16 @@
 
     def pack(k):
         packed = jnp.dot(place_hot[k], unit[...], preferred_element_type=jnp.float32).astype(jnp.bfloat16)
-        if k == 0:
-            zin[0] = packed
-        else:
-            zout[POS[k]] = packed
-            send(zout.at[POS[k]], zin.at[POS[NZ - k]], zs.at[0], zr.at[0 if k in (1, 7) else 1], at_z(k))
+        zout[POS[k]] = packed
+        send(zout.at[POS[k]], zin.at[POS[NZ - k]], zs.at[0], zr.at[0 if k in (1, 7) else 1], at_z(k))
 
     pack(1)
     pack(7)
     left = jnp.where(
-        far_row & (lax.broadcasted_iota(jnp.int32, (NXY, ROWS), 0) == dxy), local, 0.0).astype(jnp.bfloat16)
+        (far_row | (dz == 0)) & (lax.broadcasted_iota(jnp.int32, (NXY, ROWS), 0) == dxy), local, 0.0).astype(jnp.bfloat16)
     right = hot(lax.broadcasted_iota(jnp.int32, (128, ROWS), 0) == far_lane)
     ids = lax.dot_general(left, right, NT, preferred_element_type=jnp.float32)
-    for d in range(NXY):
+    for d in AROUND:
         if d == 0:
             fid_in[0] = ids[0:1, :]
         else:
@@ -192,7 +192,7 @@
     def pack_far(e):
         count = FAR_SETS[e][2]
         packed = jnp.dot(far_hot[e], unit[...], preferred_element_type=jnp.float32)
-        for d in range(NXY):
+        for d in AROUND:
             block = packed[count * d:count * d + count, :].astype(jnp.bfloat16)
             if d == 0:
                 fin[e][0] = block
@@ -202,35 +202,29 @@
 
     pack_far(0)
     pack_far(1)
-    for k in NEAR + (0,):
+    for k in NEAR:
         meta = lax.dot_general(values, place_hot[k], NT, preferred_element_type=jnp.float32)
-        if k == 0:
-            min_[0] = meta
-        else:
-            mout[POS[k]] = meta
-            send(mout.at[POS[k]], min_.at[POS[NZ - k]], ms.at[0], mr.at[0 if k in (1, 7) else 1], at_z(k))
+        mout[POS[k]] = meta
+        send(mout.at[POS[k]], min_.at[POS[NZ - k]], ms.at[0], mr.at[0], at_z(k))
     pack(2)
     pack(6)
-    pack(0)
 
     p_copies = {}
 
     def forward(g):
         members, _, count = GROUPS[g]
         total = None
-        if g == 0:
-            arrived(min_.at[pl.ds(1, 2)], mr.at[0])
         for m, k in enumerate(members):
             meta = min_[POS[k]]
             valid = meta[0:1, :] > 0.5
             there = jnp.where(valid, meta[1:2, :] * float(count) + meta[2:3, :] + float(CAP * m), -1.0)
             there = there.astype(jnp.int32)
             want = lax.broadcasted_iota(jnp.int32, (NXY * count, ROOM), 0)
-            if m == g ^ 1:
-                arrived(zin.at[pl.ds(1 + 2 * g, 2)], zr.at[g])
+            if m == 0:
+                arrived(zin.at[pl.ds(2 * g, 2)], zr.at[g])
             part = jnp.dot(hot(want == there), zin[POS[k]], preferred_element_type=jnp.float32)
             total = part if total is None else total + part
-        for d in range(NXY):
+        for d in AROUND:
             block = total[count * d:count * d + count, :].astype(jnp.bfloat16)
             if d == 0:
                 rows[g][0] = block
@@ -244,16 +238,16 @@
 
     def share_far(kk):
         arrived(z_far.at[kk], zr.at[2 + kk])
-        p_copies[2 + kk] = send(z_far.at[kk], z_far_p.at[kk], ps.at[2 + kk], pr.at[2 + kk], partner)
+        p_copies[3 + kk] = send(z_far.at[kk], z_far_p.at[kk], ps.at[3 + kk], pr.at[3 + kk], partner)
 
     arrived(fid_in.at[others], vr.at[0])
     known = jnp.concatenate([fid_in[j] for j in range(NXY)], axis=0).astype(jnp.bfloat16)
     back_at = jnp.zeros((NXY, 128), jnp.float32)
     far_values, far_places = [], []
-    for planes, first, count, factor, shift in FAR_SETS:
+    for planes, first, count in FAR_SETS:
         width = NXY * count
         flat = lax.broadcasted_iota(jnp.int32, (1, width), 1)
-        holder = (flat * factor) >> shift
+        holder = (flat * 2731) >> 16
         within = flat - holder * count
         lane = jnp.where(within < CAP * len(planes), within + CAP * first, -1)
         spread = hot(lax.broadcasted_iota(jnp.int32, (128, width), 0) == lane)
@@ -279,7 +273,7 @@
     back_at = back_at.astype(jnp.int32)
 
     def relay_far(e):
-        planes, _, count, _, _ = FAR_SETS[e]
+        planes, _, count = FAR_SETS[e]
         width = NXY * count
         chosen = []
         for m, k in enumerate(planes):
@@ -287,7 +281,7 @@
             chosen.append(hot(want == far_places[e][m:m + 1, :]))
             mout[POS[k]] = lax.dot_general(far_values[e], chosen[m], NT, preferred_element_type=jnp.float32)
             there = FAR.index(NZ - k)
-            send(mout.at[POS[k]], min_.at[POS[NZ - k]], ms.at[0], mr.at[2 + there], at_z(k))
+            send(mout.at[POS[k]], min_.at[POS[NZ - k]], ms.at[0], mr.at[1 + there], at_z(k))
         arrived(fin[e].at[others], wr.at[e])
         for m, k in enumerate(planes):
             zout[POS[k]] = jnp.dot(
@@ -295,44 +289,46 @@
             there = FAR.index(NZ - k)
             send(zout.at[POS[k]], z_far.at[there], zs.at[0], zr.at[2 + there], at_z(k))
 
-    forward(0)
-    relay_far(0)
-
-    arrived(min_.at[pl.ds(3, 2)], mr.at[1])
+    arrived(min_.at[pl.ds(0, 4)], mr.at[0])
     ids = jnp.zeros((NXY, 128), jnp.float32)
-    for k in (0,) + NEAR:
+    for k in NEAR:
         meta = min_[POS[k]]
         valid = meta[0:1, :] > 0.5
         to = jnp.where(valid, meta[1:2, :], -1.0).astype(jnp.int32)
         place_k = meta[2:3, :].astype(jnp.int32) + LANE[k]
         left = jnp.where(sub16 == to, meta[0:1, :], 0.0).astype(jnp.bfloat16)
         ids = ids + lax.dot_general(left, hot(sub128 == place_k), NT, preferred_element_type=jnp.float32)
-    for d in range(NXY):
+    for d in AROUND:
         if d == 0:
             idin[0] = ids[0:1, :]
         else:
             idout[d] = ids[d:d + 1, :]
             send(idout.at[d], idin.at[neg(d)], ids_s.at[0], ids_r.at[0], at_xy(d))
 
+    forward(0)
+    relay_far(0)
+
     forward(1)
     relay_far(1)
 
-    share(0)
+    p_copies[OWN] = send(rows[OWN], rows_p[OWN], ps.at[OWN], pr.at[OWN], partner)
     arrived(idin.at[others], ids_r.at[0])
     for j in range(NXY):
         line = idin[j]
         line = jnp.where(line < 0.5, -1.0, line)
         turned = jnp.broadcast_to(line, (128, 128)).T
-        for g, (_, base, count) in enumerate(GROUPS):
+        for g, (_, base, count) in enumerate(GROUPS[:OWN]):
             idkey[g][count * j:count * j + count, :] = turned[base:base + count, :]
-
-    for g in range(2):
+        line = fid_in[j]
+        line = jnp.where((line < 0.5) | (lane128[0:1, :] < 3 * CAP), -1.0, line)
+        idkey[OWN][24 * j:24 * j + 24, :] = jnp.broadcast_to(line, (128, 128)).T[2 * CAP:4 * CAP, :]
+    for g in range(3):
         half = WIDTH[g] // 2
         for h in range(-(-half // 128)):
             size = min(128, half - 128 * h)
             block = idkey[g][pl.ds(pl.multiple_of(half * c + 128 * h, 8), size), :]
             idq[g, :, 128 * h:128 * h + size] = block.T[0:8, :]
-    for ref in (top, top_far, acc0, acc1, acc_far):
+    for ref in (top, top_far, acc0, acc1, acc2, acc_far):
         ref[...] = jnp.full(ref.shape, -float(D), jnp.float32)
     sub256 = lax.broadcasted_iota(jnp.int32, (CLUSTERS, 128), 0).astype(jnp.float32) + 1.0
 
@@ -361,11 +357,11 @@
     def nt(a, b):
         return lax.dot_general(a, b, NT, preferred_element_type=jnp.float32)
 
-    def score_near(e):
-        pairs = [(e, e)] + [pair for g in range(e) for pair in ((g, e), (e, g))]
-        own = [nt(keys_of(kg)[0], own_half(qg)[0]) for kg, qg in pairs]
-        p_copies[e].wait_recv()
-        for (kg, qg), part in zip(pairs, own):
+    def near_own(pairs):
+        return [(pair, nt(keys_of(pair[0])[0], own_half(pair[1])[0])) for pair in pairs]
+
+    def near_finish(parts):
+        for (kg, qg), part in parts:
             nk, nq = WIDTH[kg], WIDTH[qg] // 2
             scores = part + nt(keys_of(kg)[1], own_half(qg)[1])
             for h in range(-(-nq // 128)):
@@ -381,61 +377,71 @@
 
     half_far = pl.ds(pl.multiple_of(ROOM // 2 * c, ROOM // 2), ROOM // 2)
 
-    def score_far(planes):
-        first, width = planes[0], ROOM * len(planes)
-        cut = slice(first, first + len(planes))
-        groups = [0, 1] + [2 + kk for kk in range(first + len(planes))]
-
-        def side(g):
-            if g < 2:
-                return own_half(g)
-            return z_far[g - 2, half_far, :], z_far_p[g - 2, half_far, :]
-
-        columns = z_far[cut].reshape(width, HALF)
-        own = [nt(side(g)[0], columns) for g in groups]
-        for kk in planes:
-            p_copies[2 + kk].wait_recv()
-        columns = z_far_p[cut].reshape(width, HALF)
-        for g, part in zip(groups, own):
+    def side(g):
+        if g < 3:
+            return own_half(g)
+        return z_far[g - 3, half_far, :], z_far_p[g - 3, half_far, :]
+
+    def far_own(groups, planes):
+        columns = z_far[planes[0]:planes[0] + len(planes)].reshape(ROOM * len(planes), HALF)
+        return [(g, nt(side(g)[0], columns)) for g in groups]
+
+    def far_finish(parts, planes):
+        first = planes[0]
+        columns = z_far_p[first:first + len(planes)].reshape(ROOM * len(planes), HALF)
+        for g, part in parts:
             scores = part + nt(side(g)[1], columns)
             n = scores.shape[0]
-            if g < 2:
+            if g < 3:
                 mine = idkey[g][pl.ds(pl.multiple_of(n * c, 8), n), :]
             else:
-                mine = ik_far[g - 2, half_far, :]
+                mine = ik_far[g - 3, half_far, :]
             for kk in planes:
                 line = min_[POS[FAR[kk]]][0:1, :]
                 same = mine == line
-                if g == 2 + kk:
+                if g == 3 + kk:
                     apart = (lax.broadcasted_iota(jnp.int32, (n, ROOM), 1)
                              - lax.broadcasted_iota(jnp.int32, (n, ROOM), 0))
                     same = same & (apart != n * c)
                 kept = jnp.where(same, scores[:, ROOM * (kk - first):ROOM * (kk - first) + ROOM], -float(D))
                 top_far[kk] = jnp.maximum(top_far[kk], jnp.max(kept.reshape(n // 8, 8, ROOM), axis=0))
-                if g < 2:
+                if g < 3:
                     acc[g][...] = jnp.maximum(acc[g][...], kept)
-                elif g - 2 < first:
-                    acc_far[g - 2] = jnp.maximum(acc_far[g - 2], kept)
+                elif g - 3 < first:
+                    acc_far[g - 3] = jnp.maximum(acc_far[g - 3], kept)
 
     def take_far(kk):
-        arrived(min_.at[POS[FAR[kk]]], mr.at[2 + kk])
+        arrived(min_.at[POS[FAR[kk]]], mr.at[1 + kk])
         line = min_[POS[FAR[kk]]][0:1, :]
         ik_far[kk] = jnp.broadcast_to(jnp.where(line < 0.5, -1.0, line), (128, 128)).T
         share_far(kk)
 
-    counts, total = near_sums(0)
+    counts, total = near_sums(OWN)
     sums[...] = total
-    score_near(0)
+    parts = near_own([(2, 2)])
+    p_copies[OWN].wait_recv()
+    near_finish(parts)
+    share(0)
+    parts = near_own([(0, 0), (0, 2), (2, 0)])
+    more, total = near_sums(0)
+    counts = counts + more
+    sums[...] += total
+    p_copies[0].wait_recv()
+    near_finish(parts)
     share(1)
+    parts = near_own([(1, 1), (0, 1), (1, 0), (2, 1), (1, 2)])
     take_far(0)
     take_far(1)
-    more, total = near_sums(1)
-    counts = counts + more
-    sums[...] += total
-    score_near(1)
-    score_far((0, 1))
+    p_copies[1].wait_recv()
+    near_finish(parts)
+    parts = far_own([2, 0, 1, 3, 4], (0, 1))
+    p_copies[3].wait_recv()
+    p_copies[4].wait_recv()
+    far_finish(parts, (0, 1))
     take_far(2)
-    score_far((2,))
+    parts = far_own([2, 0, 1, 3, 4, 5], (2,))
+    p_copies[5].wait_recv()
+    far_finish(parts, (2,))
     for g, (_, base, count) in enumerate(GROUPS):
         half = WIDTH[g] // 2
         pieces = []
@@ -482,10 +488,12 @@
         best_copy(i, False).start()
         best_copy(i, True).start()
 
+    more, total = near_sums(1)
+    counts = counts + more
     for kk in range(3):
         more, part = member_sums(ik_far[kk], z_far[kk])
         counts = counts + more
-        total = part if kk == 0 else total + part
+        total = total + part
     cent_load.wait()
     mass_load.wait()
     number = jnp.sum(counts, axis=1, keepdims=True)
@@ -505,7 +513,7 @@
     back = {}
     for k in (2, 6, 1, 7):
         back[NZ - k] = send(
-            ret1, ret2.at[POS[NZ - k] - 1], fs.at[POS[k] - 1], fr.at[POS[NZ - k] - 1], at_z(k))
+            ret1, ret2.at[POS[NZ - k]], fs.at[POS[k]], fr.at[POS[NZ - k]], at_z(k))
     arrived(far_z, ur.at[0])
     lane16 = lax.broadcasted_iota(jnp.int32, (NXY, 128), 1)
     got = jnp.zeros((NXY, 128), jnp.float32)
@@ -521,7 +529,7 @@
         for kk in range(3):
             far_over = jnp.maximum(far_over, far_z[h, kk][:, 128:256])
     got = jnp.where(lane16 == 127, far_over, got)
-    for j in range(NXY):
+    for j in AROUND:
         if j == 0:
             far_ret[0] = got[0:1, :]
         else:
@@ -541,7 +549,7 @@
     for k in NEAR:
         back[k].wait_recv()
         for j in range(NXY):
-            result, flag = pick(ret2[POS[k] - 1, j], k * NXY + j, result, flag)
+            result, flag = pick(ret2[POS[k], j], k * NXY + j, result, flag)
     arrived(far_ret.at[others], tr.at[0])
     for d in range(NXY):
         result, flag = pick(far_ret[d], NZ * NXY + d, result, flag)
@@ -560,8 +568,8 @@
     sent(best_out, bs.at[1])
     for copy in list(back.values()) + list(p_copies.values()):
         copy.wait_send()
-    sent(zout.at[pl.ds(1, NZ - 1)], zs.at[0])
-    sent(mout.at[pl.ds(1, NZ - 1)], ms.at[0])
+    sent(zout, zs.at[0])
+    sent(mout, ms.at[0])
     for e in range(2):
         sent(xout[e].at[others], xs.at[e])
         sent(fout[e].at[others], ws.at[e])
@@ -592,25 +600,26 @@
             pltpu.VMEM((ROWS, HALF), bf16),
             pltpu.VMEM((1, ROWS), f32),
             pltpu.VMEM((1, ROWS), f32),
-            pltpu.VMEM((NZ, ROOM, HALF), bf16),
-            pltpu.VMEM((1 + len(NEAR), ROOM, HALF), bf16),
+            pltpu.VMEM((NZ - 1, ROOM, HALF), bf16),
+            pltpu.VMEM((len(NEAR), ROOM, HALF), bf16),
             pltpu.VMEM((3, ROOM, HALF), bf16),
             pltpu.VMEM((3, ROOM, HALF), bf16),
-            pltpu.VMEM((NZ, 8, 128), f32),
-            pltpu.VMEM((NZ, 8, 128), f32),
-            *[pltpu.VMEM((NXY, count, HALF), bf16) for _, _, count in GROUPS],
+            pltpu.VMEM((NZ - 1, 8, 128), f32),
+            pltpu.VMEM((NZ - 1, 8, 128), f32),
+            *[pltpu.VMEM((NXY, count, HALF), bf16) for _, _, count in GROUPS[:OWN]],
             pltpu.VMEM((NXY, *line), f32),
             *[pltpu.VMEM((NXY, far[2], HALF), bf16) for far in FAR_SETS],
             *[pltpu.VMEM((NXY, far[2], HALF), bf16) for far in FAR_SETS],
+            pltpu.VMEM((NXY, FAR_SETS[1][2], HALF), bf16),
             pltpu.VMEM((NXY, *line), f32),
             pltpu.VMEM((NXY, *line), f32),
-            *[pltpu.VMEM((NXY, count, HALF), bf16) for _, _, count in GROUPS],
-            *[pltpu.VMEM((NXY, count, HALF), bf16) for _, _, count in GROUPS],
+            *[pltpu.VMEM((NXY, count, HALF), bf16) for _, _, count in GROUPS[:OWN]],
+            *[pltpu.VMEM((NXY, count, HALF), bf16) for _, _, count in GROUPS[:OWN]],
             pltpu.VMEM((NXY, *line), f32),
             *[pltpu.VMEM((NXY * count, 128), f32) for _, _, count in GROUPS],
             pltpu.VMEM((3, 128, 128), f32),
-            pltpu.VMEM((2, 8, 384), f32),
-            pltpu.VMEM((2, 8, 384), f32),
+            pltpu.VMEM((3, 8, 256), f32),
+            pltpu.VMEM((3, 8, 256), f32),
             *[pltpu.VMEM((width // 2, 128), f32) for width in WIDTH],
             pltpu.VMEM((2, ROOM // 2, 128), f32),
             pltpu.VMEM((3, 8, 128), f32),
@@ -627,8 +636,8 @@
             pltpu.VMEM((CLUSTERS, HALF), f32),
             pltpu.VMEM((ROWS,), i32),
             pltpu.VMEM((1, CLUSTERS), f32),
-            dma((5,)), dma((2,)), dma((1,)), dma((5,)), dma((1,)), dma((5,)), dma((2,)), dma((2,)),
-            dma((1,)), dma((1,)), dma((5,)), dma((5,)), dma((2,)), dma((1,)), dma((4,)), dma((4,)),
+            dma((5,)), dma((2,)), dma((1,)), dma((5,)), dma((1,)), dma((4,)), dma((2,)), dma((2,)),
+            dma((1,)), dma((1,)), dma((6,)), dma((6,)), dma((2,)), dma((1,)), dma((4,)), dma((4,)),
             dma((2,)), dma((2,)), dma((1,)), dma((1,)), dma((2,)), dma((1,)), dma((1,)), dma((1,)),
         ],
         compiler_params=pltpu.CompilerParams(

time: 54 us -> 53.3 us (0.987)
  Pallas kernels: 51.5 us -> 50.7 us
    pallas_call x1, Pallas kernels: 51.5 us -> 50.7 us  [compact(): pl.pallas_call(exchange_kernel, out_shape=(jax.ShapeDtypeStruct((1, ROWS)...]
where the time goes in v5:
time: 53.3 us; the launch traced here: 53.2 us
  Pallas kernels  50.7 us (95%)
  between operations  1.41 us (3%)
  local copies, waits for them, and re-layouts  0.82 us (2%)
    pallas_call x1, Pallas kernels, compact(): pl.pallas_call(exchange_kernel, out_shape=(jax.ShapeDtypeStruct((1, ROWS)...  50.7 us

profile of v5, /device:TPU:1, one launch (start us, length us, event | category | flops | bytes accessed | tf_op | source)
XLA Modules:
  0.0 53.2 jit_solution(4311514407894364518)
XLA Ops:
  0.6 0.0 copy-start
  0.6 0.0 copy-start.2
  0.7 0.0 copy-start.1
  0.7 0.0 copy-start.3
  0.7 50.7 %shard_map.61 = (f32[1,768]{1,0:T(1,128)S(1)}, f32[256,512]{1,0:T(8,128)S(1)}, s32[1,1]{1,0:T(1,128)}) custom-call(f32[768,512]{1,0:T(8,128)} %emb_ref.1, s32[768]{0:T(1024)} %cid_ref.1, f32[256,512]{1,0:T(8,128)} %cent_ref.1, f32[1,256]{1,0:T(1,128)} %bitcast.9), custom_call_target="tpu_custom_call" | custom-call | tf_op jit(solution)/shard_map/pallas_call | solution.py:589
  52.1 0.0 copy-done
  52.1 0.0 copy-done.2
  52.1 0.0 copy-done.1
  52.1 0.0 copy-done.3
  52.1 0.3 conditional.1
  52.4 0.0 copy-start.4
  52.4 0.8 %copy.19 = f32[256,512]{1,0:T(8,128)} copy(f32[256,512]{1,0:T(8,128)S(1)} %get-tuple-element.41) | data formatting | bytes 1048576
  53.2 0.0 copy-done.4
  (1 shorter events, 0.0 us)
Async XLA Ops:
  0.6 51.4 %copy-start = (f32[768,512]{1,0:T(8,128)S(1)}, f32[768,512]{1,0:T(8,128)}, u32[]{:S(2)}) copy-start(f32[768,512]{1,0:T(8,128)} %emb_ref.1) | copy-start | bytes 4718596
  0.6 51.4 %copy-start.2 = (s32[768]{0:T(1024)S(1)}, s32[768]{0:T(1024)}, u32[]{:S(2)}) copy-start(s32[768]{0:T(1024)} %cid_ref.1) | copy-start | bytes 9220
  0.7 51.4 %copy-start.1 = (f32[256,512]{1,0:T(8,128)S(1)}, f32[256,512]{1,0:T(8,128)}, u32[]{:S(2)}) copy-start(f32[256,512]{1,0:T(8,128)} %cent_ref.1) | copy-start | bytes 1572868
  0.7 51.4 %copy-start.3 = (f32[256]{0:T(256)S(1)}, f32[256]{0:T(256)}, u32[]{:S(2)}) copy-start(f32[256]{0:T(256)} %param.9) | copy-start | bytes 3076
  52.4 0.8 %copy-start.4 = (f32[768]{0:T(1024)}, f32[768]{0:T(1024)S(1)}, u32[]{:S(2)}) copy-start(f32[768]{0:T(1024)S(1)} %get-tuple-element.40) | copy-start | bytes 9220

commit v6 on v5

--- a/solution.py
+++ b/solution.py
@@ -442,17 +442,6 @@
     parts = far_own([2, 0, 1, 3, 4, 5], (2,))
     p_copies[5].wait_recv()
     far_finish(parts, (2,))
-    for g, (_, base, count) in enumerate(GROUPS):
-        half = WIDTH[g] // 2
-        pieces = []
-        for h in range(-(-half // 128)):
-            size = min(128, half - 128 * h)
-            best = jnp.max(top[g, :, 128 * h:128 * h + size], axis=0, keepdims=True)
-            pieces.append(jnp.broadcast_to(best, (128, size)).T)
-        best = jnp.concatenate(pieces, axis=0)
-        best = jnp.maximum(best, jnp.max(acc[g][...], axis=1, keepdims=True)) * (1.0 / D)
-        for i in range(NXY // 2):
-            column[i, base:base + count, :] = best[count * i:count * i + count, :]
     for kk in range(3):
         best = jnp.max(top_far[kk], axis=0, keepdims=True)
         if kk < 2:
@@ -465,6 +454,17 @@
         there = FAR.index(NZ - k)
         for core in range(2):
             send(far_out.at[kk], far_z.at[c, there], us.at[core], ur.at[0], (at_z(k)[0], core))
+    for g, (_, base, count) in enumerate(GROUPS):
+        half = WIDTH[g] // 2
+        pieces = []
+        for h in range(-(-half // 128)):
+            size = min(128, half - 128 * h)
+            best = jnp.max(top[g, :, 128 * h:128 * h + size], axis=0, keepdims=True)
+            pieces.append(jnp.broadcast_to(best, (128, size)).T)
+        best = jnp.concatenate(pieces, axis=0)
+        best = jnp.maximum(best, jnp.max(acc[g][...], axis=1, keepdims=True)) * (1.0 / D)
+        for i in range(NXY // 2):
+            column[i, base:base + count, :] = best[count * i:count * i + count, :]
     for i in range(NXY // 2):
         best_out[i] = jnp.where(last, over, column[i].T[0:1, :])
 
@@ -502,18 +502,6 @@
     nc_copy = pltpu.make_async_copy(cent, nc_ref, local_sem.at[2])
     nc_copy.start()
 
-    @pl.when(c == 0)
-    def _():
-        arrived(ret1.at[others], br.at[0])
-
-    @pl.when(c == 1)
-    def _():
-        arrived(ret1, br.at[0])
-
-    back = {}
-    for k in (2, 6, 1, 7):
-        back[NZ - k] = send(
-            ret1, ret2.at[POS[NZ - k]], fs.at[POS[k]], fr.at[POS[NZ - k]], at_z(k))
     arrived(far_z, ur.at[0])
     lane16 = lax.broadcasted_iota(jnp.int32, (NXY, 128), 1)
     got = jnp.zeros((NXY, 128), jnp.float32)
@@ -535,6 +523,18 @@
         else:
             back_out[j] = got[j:j + 1, :]
             send(back_out.at[j], far_ret.at[neg(j)], ts.at[0], tr.at[0], at_xy(j))
+    @pl.when(c == 0)
+    def _():
+        arrived(ret1.at[others], br.at[0])
+
+    @pl.when(c == 1)
+    def _():
+        arrived(ret1, br.at[0])
+
+    back = {}
+    for k in (2, 6, 1, 7):
+        back[NZ - k] = send(
+            ret1, ret2.at[POS[NZ - k]], fs.at[POS[k]], fr.at[POS[NZ - k]], at_z(k))
     tile_t = tiles_i[0]
     lane_t = tiles_i[1]
     result = jnp.zeros((8, 128), jnp.float32)

time: 53.3 us -> 53.2 us (level)
  no operation moved by 1% of the time
where the time goes in v6:
time: 53.2 us; the launch traced here: 53.1 us
  Pallas kernels  50.6 us (95%)
  between operations  1.41 us (3%)
  local copies, waits for them, and re-layouts  0.82 us (2%)
    pallas_call x1, Pallas kernels, compact(): pl.pallas_call(exchange_kernel, out_shape=(jax.ShapeDtypeStruct((1, ROWS)...  50.6 us

profile of v6, /device:TPU:1, one launch (start us, length us, event | category | flops | bytes accessed | tf_op | source)
XLA Modules:
  0.0 53.1 jit_solution(7900650607176388389)
XLA Ops:
  0.6 0.0 copy-start
  0.6 0.0 copy-start.2
  0.7 0.0 copy-start.1
  0.7 0.0 copy-start.3
  0.7 50.6 %shard_map.61 = (f32[1,768]{1,0:T(1,128)S(1)}, f32[256,512]{1,0:T(8,128)S(1)}, s32[1,1]{1,0:T(1,128)}) custom-call(f32[768,512]{1,0:T(8,128)} %emb_ref.1, s32[768]{0:T(1024)} %cid_ref.1, f32[256,512]{1,0:T(8,128)} %cent_ref.1, f32[1,256]{1,0:T(1,128)} %bitcast.9), custom_call_target="tpu_custom_call" | custom-call | tf_op jit(solution)/shard_map/pallas_call | solution.py:589
  52.0 0.0 copy-done
  52.0 0.0 copy-done.2
  52.0 0.0 copy-done.1
  52.0 0.0 copy-done.3
  52.0 0.3 conditional.1
  52.3 0.0 copy-start.4
  52.3 0.8 %copy.19 = f32[256,512]{1,0:T(8,128)} copy(f32[256,512]{1,0:T(8,128)S(1)} %get-tuple-element.41) | data formatting | bytes 1048576
  53.1 0.0 copy-done.4
  (1 shorter events, 0.0 us)
Async XLA Ops:
  0.6 51.3 %copy-start = (f32[768,512]{1,0:T(8,128)S(1)}, f32[768,512]{1,0:T(8,128)}, u32[]{:S(2)}) copy-start(f32[768,512]{1,0:T(8,128)} %emb_ref.1) | copy-start | bytes 4718596
  0.6 51.3 %copy-start.2 = (s32[768]{0:T(1024)S(1)}, s32[768]{0:T(1024)}, u32[]{:S(2)}) copy-start(s32[768]{0:T(1024)} %cid_ref.1) | copy-start | bytes 9220
  0.7 51.3 %copy-start.1 = (f32[256,512]{1,0:T(8,128)S(1)}, f32[256,512]{1,0:T(8,128)}, u32[]{:S(2)}) copy-start(f32[256,512]{1,0:T(8,128)} %cent_ref.1) | copy-start | bytes 1572868
  0.7 51.3 %copy-start.3 = (f32[256]{0:T(256)S(1)}, f32[256]{0:T(256)}, u32[]{:S(2)}) copy-start(f32[256]{0:T(256)} %param.9) | copy-start | bytes 3076
  52.3 0.8 %copy-start.4 = (f32[768]{0:T(1024)}, f32[768]{0:T(1024)S(1)}, u32[]{:S(2)}) copy-start(f32[768]{0:T(1024)S(1)} %get-tuple-element.40) | copy-start | bytes 9220

commit v7 on v6

--- a/solution.py
+++ b/solution.py
@@ -201,13 +201,13 @@
                 send(fout[e].at[d], fin[e].at[neg(d)], ws.at[e], wr.at[e], at_xy(d))
 
     pack_far(0)
-    pack_far(1)
     for k in NEAR:
         meta = lax.dot_general(values, place_hot[k], NT, preferred_element_type=jnp.float32)
         mout[POS[k]] = meta
         send(mout.at[POS[k]], min_.at[POS[NZ - k]], ms.at[0], mr.at[0], at_z(k))
     pack(2)
     pack(6)
+    pack_far(1)
 
     p_copies = {}
 

time: 53.2 us -> 53.2 us (level)
  no operation moved by 1% of the time
where the time goes in v7:
time: 53.2 us; the launch traced here: 53.1 us
  Pallas kernels  50.6 us (95%)
  between operations  1.41 us (3%)
  local copies, waits for them, and re-layouts  0.82 us (2%)
    pallas_call x1, Pallas kernels, compact(): pl.pallas_call(exchange_kernel, out_shape=(jax.ShapeDtypeStruct((1, ROWS)...  50.6 us

profile of v7, /device:TPU:1, one launch (start us, length us, event | category | flops | bytes accessed | tf_op | source)
XLA Modules:
  0.0 53.1 jit_solution(1113429187499380567)
XLA Ops:
  0.6 0.0 copy-start
  0.6 0.0 copy-start.2
  0.7 0.0 copy-start.1
  0.7 0.0 copy-start.3
  0.7 50.6 %shard_map.61 = (f32[1,768]{1,0:T(1,128)S(1)}, f32[256,512]{1,0:T(8,128)S(1)}, s32[1,1]{1,0:T(1,128)}) custom-call(f32[768,512]{1,0:T(8,128)} %emb_ref.1, s32[768]{0:T(1024)} %cid_ref.1, f32[256,512]{1,0:T(8,128)} %cent_ref.1, f32[1,256]{1,0:T(1,128)} %bitcast.9), custom_call_target="tpu_custom_call" | custom-call | tf_op jit(solution)/shard_map/pallas_call | solution.py:589
  52.0 0.0 copy-done
  52.0 0.0 copy-done.2
  52.0 0.0 copy-done.1
  52.0 0.0 copy-done.3
  52.0 0.3 conditional.1
  52.3 0.0 copy-start.4
  52.3 0.8 %copy.19 = f32[256,512]{1,0:T(8,128)} copy(f32[256,512]{1,0:T(8,128)S(1)} %get-tuple-element.41) | data formatting | bytes 1048576
  53.1 0.0 copy-done.4
  (1 shorter events, 0.0 us)
Async XLA Ops:
  0.6 51.3 %copy-start = (f32[768,512]{1,0:T(8,128)S(1)}, f32[768,512]{1,0:T(8,128)}, u32[]{:S(2)}) copy-start(f32[768,512]{1,0:T(8,128)} %emb_ref.1) | copy-start | bytes 4718596
  0.6 51.3 %copy-start.2 = (s32[768]{0:T(1024)S(1)}, s32[768]{0:T(1024)}, u32[]{:S(2)}) copy-start(s32[768]{0:T(1024)} %cid_ref.1) | copy-start | bytes 9220
  0.7 51.3 %copy-start.1 = (f32[256,512]{1,0:T(8,128)S(1)}, f32[256,512]{1,0:T(8,128)}, u32[]{:S(2)}) copy-start(f32[256,512]{1,0:T(8,128)} %cent_ref.1) | copy-start | bytes 1572868
  0.7 51.3 %copy-start.3 = (f32[256]{0:T(256)S(1)}, f32[256]{0:T(256)}, u32[]{:S(2)}) copy-start(f32[256]{0:T(256)} %param.9) | copy-start | bytes 3076
  52.3 0.8 %copy-start.4 = (f32[768]{0:T(1024)}, f32[768]{0:T(1024)S(1)}, u32[]{:S(2)}) copy-start(f32[768]{0:T(1024)S(1)} %get-tuple-element.40) | copy-start | bytes 9220

commit v8 on v7

--- a/solution.py
+++ b/solution.py
@@ -207,7 +207,6 @@
         send(mout.at[POS[k]], min_.at[POS[NZ - k]], ms.at[0], mr.at[0], at_z(k))
     pack(2)
     pack(6)
-    pack_far(1)
 
     p_copies = {}
 
@@ -289,6 +288,7 @@
             there = FAR.index(NZ - k)
             send(zout.at[POS[k]], z_far.at[there], zs.at[0], zr.at[2 + there], at_z(k))
 
+    pack_far(1)
     arrived(min_.at[pl.ds(0, 4)], mr.at[0])
     ids = jnp.zeros((NXY, 128), jnp.float32)
     for k in NEAR:

time: 53.2 us -> 53.2 us (level)
  no operation moved by 1% of the time
where the time goes in v8:
time: 53.2 us; the launch traced here: 53.1 us
  Pallas kernels  50.6 us (95%)
  between operations  1.41 us (3%)
  local copies, waits for them, and re-layouts  0.82 us (2%)
    pallas_call x1, Pallas kernels, compact(): pl.pallas_call(exchange_kernel, out_shape=(jax.ShapeDtypeStruct((1, ROWS)...  50.6 us

profile of v8, /device:TPU:1, one launch (start us, length us, event | category | flops | bytes accessed | tf_op | source)
XLA Modules:
  0.0 53.1 jit_solution(8725800051907282004)
XLA Ops:
  0.6 0.0 copy-start
  0.6 0.0 copy-start.2
  0.7 0.0 copy-start.1
  0.7 0.0 copy-start.3
  0.7 50.6 %shard_map.61 = (f32[1,768]{1,0:T(1,128)S(1)}, f32[256,512]{1,0:T(8,128)S(1)}, s32[1,1]{1,0:T(1,128)}) custom-call(f32[768,512]{1,0:T(8,128)} %emb_ref.1, s32[768]{0:T(1024)} %cid_ref.1, f32[256,512]{1,0:T(8,128)} %cent_ref.1, f32[1,256]{1,0:T(1,128)} %bitcast.9), custom_call_target="tpu_custom_call" | custom-call | tf_op jit(solution)/shard_map/pallas_call | solution.py:589
  52.0 0.0 copy-done
  52.0 0.0 copy-done.2
  52.0 0.0 copy-done.1
  52.0 0.0 copy-done.3
  52.0 0.3 conditional.1
  52.3 0.0 copy-start.4
  52.3 0.8 %copy.19 = f32[256,512]{1,0:T(8,128)} copy(f32[256,512]{1,0:T(8,128)S(1)} %get-tuple-element.41) | data formatting | bytes 1048576
  53.1 0.0 copy-done.4
  (1 shorter events, 0.0 us)
Async XLA Ops:
  0.6 51.3 %copy-start = (f32[768,512]{1,0:T(8,128)S(1)}, f32[768,512]{1,0:T(8,128)}, u32[]{:S(2)}) copy-start(f32[768,512]{1,0:T(8,128)} %emb_ref.1) | copy-start | bytes 4718596
  0.6 51.3 %copy-start.2 = (s32[768]{0:T(1024)S(1)}, s32[768]{0:T(1024)}, u32[]{:S(2)}) copy-start(s32[768]{0:T(1024)} %cid_ref.1) | copy-start | bytes 9220
  0.7 51.3 %copy-start.1 = (f32[256,512]{1,0:T(8,128)S(1)}, f32[256,512]{1,0:T(8,128)}, u32[]{:S(2)}) copy-start(f32[256,512]{1,0:T(8,128)} %cent_ref.1) | copy-start | bytes 1572868
  0.7 51.3 %copy-start.3 = (f32[256]{0:T(256)S(1)}, f32[256]{0:T(256)}, u32[]{:S(2)}) copy-start(f32[256]{0:T(256)} %param.9) | copy-start | bytes 3076
  52.3 0.8 %copy-start.4 = (f32[768]{0:T(1024)}, f32[768]{0:T(1024)S(1)}, u32[]{:S(2)}) copy-start(f32[768]{0:T(1024)S(1)} %get-tuple-element.40) | copy-start | bytes 9220
